TPU v7x, 256 devices: a whole 4x4x8 slice. The times are simulated.
256 devices in a mesh: rows: 128 (over x, y, z), sub: 2 (over core).
Axes of the slice: x: 4, y: 4, z: 8, core: 2. Of those that a mesh axis runs over, the one named last changes fastest.
Arguments:
- tokens_x: bfloat16 [16384, 6144], P(('rows', 'sub')), may hold values from -24 to 24
- test_matrix: bfloat16 [96, 6144], replicated, may hold values from -0.078125 to 0.078125
Outputs:
- basis: float32 [16384, 96], P(('rows', 'sub'))
- projected: float32 [6144, 96], P(('rows', 'sub'))
All inputs are finite; a program needn't handle non-finite values.
Results may differ from a plain program's by a relative error of at most 0.012.
The roundings to bfloat16 on the way count: a program that leaves them out, or rounds other values in their place, can miss the bound.
Values may be sent and summed in bfloat16 or wider, within the bound.
No kernel may reach another device: no remote copies, remote signals or barrier semaphores. Data moves between devices by JAX's collectives and lax.ppermute only.
A program may use at most 64 MiB of HBM per device.

v0:
```python
import jax
import jax.numpy as jnp
from jax import lax
from jax.sharding import Mesh
from jax.sharding import PartitionSpec as P

ROWS_SUB = ("rows_0", "rows_1", "rows_2", "sub")


def in_blocks(array, dim, devices):
    before, after = (array.shape[:dim], array.shape[dim + 1 :])
    return jnp.moveaxis(array.reshape(*before, devices, -1, *after), dim, 0)


def sent_and_summed(array, axis, dim):
    devices = lax.axis_size(axis)
    parts = lax.all_to_all(in_blocks(array, dim, devices), axis, 0, 0, tiled=True)
    return jnp.sum(parts, axis=0)


def sum_in_two_steps(array, axes, dim):
    far, near = axes
    own = sent_and_summed(in_blocks(array, dim, lax.axis_size(far)), near, dim + 1)
    return jnp.sum(lax.all_to_all(own, far, 0, 0, tiled=True), axis=0)


def filled_up(lines, devices):
    spare = -lines.shape[0] % devices
    if not spare:
        return lines
    return jnp.concatenate([lines, jnp.zeros((spare, *lines.shape[1:]), lines.dtype)])


def from_everyone(array, axis):
    copies = jnp.broadcast_to(array, (lax.axis_size(axis), *array.shape))
    return lax.all_to_all(copies, axis, split_axis=0, concat_axis=0, tiled=True)


def in_order(parts, dim):
    parts = jnp.moveaxis(parts, 0, dim)
    shape = parts.shape
    return parts.reshape(*shape[:dim], shape[dim] * shape[dim + 1], *shape[dim + 2 :])


def whole_of(array, axes, dim):
    far, near = axes
    leading = from_everyone(array, far)
    parts = jnp.swapaxes(from_everyone(leading, near), 0, 1)
    return in_order(parts.reshape(-1, *array.shape), dim)


def nested_sum(array, axes):
    lines = array.reshape(-1, array.shape[-1])
    own = sum_in_two_steps(
        filled_up(lines, lax.axis_size(axes[0]) * lax.axis_size(axes[1])), axes, 0
    )
    whole = whole_of(own, axes, 0)
    return whole[: len(lines)].reshape(array.shape)


def sum_in_two_steps_2(array, axes, dim):
    far, near = axes
    leading = sent_and_summed(array, far, dim)
    return sent_and_summed(leading, near, dim)


def taken_together(array, axis):
    everything = from_everyone(array, axis)
    return jnp.sum(everything, axis=0)


def by_axis(array, axes):
    far, near = axes
    return taken_together(taken_together(array, near), far)


def solve_right(factor, matrix):
    return lax.linalg.triangular_solve(
        factor, matrix, left_side=False, lower=True, transpose_a=True
    )


def symmetric(product, total):
    return (product + product.T) / (2.0 * total)


def small_product(left, right):
    return jnp.dot(
        left.astype(jnp.float32).T,
        right,
        precision=lax.Precision.HIGHEST,
        preferred_element_type=jnp.float32,
    )


def on_device(tokens_x, test_matrix):
    devices_all = lax.axis_size(ROWS_SUB)
    total = jnp.float32(tokens_x.shape[0] * devices_all)
    share = tokens_x.shape[1] // devices_all
    mine = lax.axis_index(ROWS_SUB) * share
    sketch = lax.dot_general(
        tokens_x, test_matrix, (((1,), (1,)), ((), ())), preferred_element_type=jnp.float32
    ).astype(jnp.bfloat16)
    summed = lax.dot_general(
        tokens_x, sketch, (((0,), (0,)), ((), ())), preferred_element_type=jnp.float32
    )
    cross = nested_sum(summed, ("rows_0", ("rows_1", "rows_2", "sub")))
    gram_one = symmetric(
        jnp.dot(
            test_matrix.astype(jnp.float32),
            cross,
            precision=lax.Precision.HIGHEST,
            preferred_element_type=jnp.float32,
        ),
        total,
    )
    middle = solve_right(jnp.linalg.cholesky(gram_one), cross).astype(jnp.bfloat16)
    power = jnp.dot(tokens_x, middle, preferred_element_type=jnp.float32)
    middle_mine = lax.dynamic_slice_in_dim(middle, mine, share, 0)
    rounded = power.astype(jnp.bfloat16)
    cross_two = sum_in_two_steps_2(
        lax.dot_general(
            tokens_x, rounded, (((0,), (0,)), ((), ())), preferred_element_type=jnp.float32
        ),
        ("rows_0", ("rows_1", "rows_2", "sub")),
        0,
    )
    partial_two = small_product(middle_mine, cross_two)
    gram_two = symmetric(by_axis(partial_two, (("rows_0", "rows_1"), ("rows_2", "sub"))), total)
    factor_two = jnp.linalg.cholesky(gram_two)
    basis = solve_right(factor_two, power)
    projected = solve_right(factor_two, cross_two) / jnp.sqrt(total)
    return (basis, projected)


def solution(mesh):
    finer = Mesh(
        mesh.devices.reshape(4, 4, 8, mesh.shape["sub"]), ("rows_0", "rows_1", "rows_2", "sub")
    )
    return jax.shard_map(
        on_device,
        mesh=finer,
        in_specs=(P(ROWS_SUB, None), P()),
        out_specs=(P(ROWS_SUB, None), P(ROWS_SUB, None)),
        check_vma=False,
    )
```

profile of v0, /device:TPU:1, one launch (start us, length us, event | category | flops | bytes accessed | tf_op | source)
XLA Modules:
  0.0 354.6 jit_solution(8322391391996672591)
XLA Ops:
  0.6 0.0 copy-start
  0.6 1.3 copy-done
  1.9 3.1 convolution_bitcast_fusion
  5.0 2.3 copy.32
  7.3 2.3 copy.33
  9.6 86.5 %all_to_all.40 = f32[64,4,24,96]{3,2,1,0:T(8,128)} all-to-all(f32[64,4,24,96]{3,2,1,0:T(8,128)S(1)} %copy.33), channel_id=1, replica_groups=mesh['rows_0'=4,'rows_1'=4,'rows_2'=8,'sub'=2] {'rows_1','rows_2','sub'}, dimensions={0} | all-to-all | bytes 4718592 | tf_op jit(solution)/shard_map/all_to_all | solution.py:17
  96.1 2.1 reduce_sum.54
  98.3 8.2 %all_to_all.41 = f32[4,24,96]{2,1,0:T(8,128)S(1)} all-to-all(f32[4,24,96]{2,1,0:T(8,128)S(1)} %reduce_sum.54), channel_id=1, replica_groups=mesh['rows_0'=4,'rows_1'=4,'rows_2'=8,'sub'=2] {'rows_0'}, dimensions={0} | all-to-all | bytes 73728 | tf_op jit(solution)/shard_map/all_to_all | solution.py:24
  106.5 6.7 %all_to_all.42 = f32[4,24,96]{2,1,0:T(8,128)S(1)} all-to-all(f32[4,24,96]{2,1,0:T(8,128)S(1)} %broadcast_in_dim.13), channel_id=1, replica_groups=mesh['rows_0'=4,'rows_1'=4,'rows_2'=8,'sub'=2] {'rows_0'}, dimensions={0} | all-to-all | bytes 73728 | tf_op jit(solution)/shard_map/all_to_all | solution.py:36
  113.2 0.4 broadcast_in_dim.14
  113.6 82.0 %all_to_all.43 = f32[64,4,24,96]{3,2,1,0:T(8,128)S(1)} all-to-all(f32[64,4,24,96]{3,2,1,0:T(8,128)S(1)} %broadcast_in_dim.14), channel_id=1, replica_groups=mesh['rows_0'=4,'rows_1'=4,'rows_2'=8,'sub'=2] {'rows_1','rows_2','sub'}, dimensions={0} | all-to-all | bytes 4718592 | tf_op jit(solution)/shard_map/all_to_all | solution.py:36
  195.7 0.2 copy.34
  195.9 0.0 copy-start.1
  195.9 1.7 copy-done.1
  197.5 2.6 fusion.15
  200.2 0.1 copy.35
  200.3 0.1 copy.36
  200.4 0.0 copy-start.2
  200.4 8.8 %cholesky.44 = f32[96,96]{1,0:T(8,128)S(1)} custom-call(f32[96,96]{1,0:T(8,128)S(1)} %fusion.8), custom_call_target="Cholesky" | custom-call | tf_op jit(solution)/shard_map/jit(cholesky)/cholesky | solution.py:117
  209.2 0.6 compare_reduce_fusion.1
  209.9 0.7 fusion
  210.5 7.4 %custom-call.10 = f32[1,96,96]{1,2,0:T(8,128)S(1)} custom-call(f32[1,96,96]{2,1,0:T(8,128)S(1)} %fusion), custom_call_target="InvertDiagBlocksLowerTriangular" | custom-call | tf_op jit(solution)/shard_map/triangular_solve | solution.py:78
  217.9 5.3 %convolution_convert_fusion = bf16[6144,96]{0,1:T(8,128)(2,1)S(1)} fusion(f32[6144,96]{1,0:T(8,128)} %bitcast.54, f32[1,96,96]{1,2,0:T(8,128)S(1)} %custom-call.10), kind=kOutput, calls=%fused_computation.1 | convolution fusion | flops 680067072 | bytes 3575808 | tf_op jit(solution)/shard_map/triangular_solve | solution.py:78
  223.2 0.0 copy-start.3
  223.2 1.0 copy-done.3
  224.2 0.0 copy-done.2
  224.2 0.5 fusion.16
  224.8 0.0 copy-start.4
  224.8 0.5 fusion.12
  225.3 0.1 copy-done.4
  225.4 0.2 copy.45
  225.6 31.5 %all_to_all.44 = f32[4,1536,96]{1,2,0:T(8,128)S(1)} all-to-all(f32[4,1536,96]{1,2,0:T(8,128)S(1)} %bitcast.57), channel_id=1, replica_groups=mesh['rows_0'=4,'rows_1'=4,'rows_2'=8,'sub'=2] {'rows_0'}, dimensions={0} | all-to-all | bytes 4718592 | tf_op jit(solution)/shard_map/all_to_all | solution.py:17
  257.0 1.0 reduce_sum.56
  258.0 2.3 copy.39
  260.3 6.7 %all-to-all-start.5 = ((f32[64,24,96]{2,1,0:T(8,128)}), f32[64,24,96]{2,1,0:T(8,128)S(1)}, u32[]{:S(2)}, u32[]{:S(2)}) async-start(f32[64,24,96]{2,1,0:T(8,128)} %bitcast.10), calls=%async_computation.5 | async-start | bytes 1572864 | tf_op jit(solution)/shard_map/all_to_all | solution.py:17
  267.0 22.9 %all-to-all-done.5 = f32[64,24,96]{2,1,0:T(8,128)S(1)} async-done(((f32[64,24,96]{2,1,0:T(8,128)}), f32[64,24,96]{2,1,0:T(8,128)S(1)}, u32[]{:S(2)}, u32[]{:S(2)}) %all-to-all-start.5) | async-done | bytes 589856 | tf_op jit(solution)/shard_map/all_to_all | solution.py:17
  290.0 0.1 reduce_sum.57
  290.1 1.0 fusion.10
  291.1 0.1 broadcast_in_dim.15
  291.2 27.4 %all_to_all.45 = f32[16,96,96]{2,1,0:T(8,128)S(1)} all-to-all(f32[16,96,96]{2,1,0:T(8,128)S(1)} %broadcast_in_dim.15), channel_id=1, replica_groups=mesh['rows_0'=4,'rows_1'=4,'rows_2'=8,'sub'=2] {'rows_2','sub'}, dimensions={0} | all-to-all | bytes 1179648 | tf_op jit(solution)/shard_map/all_to_all | solution.py:36
  318.6 0.0 copy-start.5
  318.6 0.1 reduce_sum.58
  318.6 0.1 broadcast_in_dim.16
  318.7 16.5 %all_to_all.46 = f32[16,96,96]{2,1,0:T(8,128)S(1)} all-to-all(f32[16,96,96]{2,1,0:T(8,128)S(1)} %broadcast_in_dim.16), channel_id=1, replica_groups=mesh['rows_0'=4,'rows_1'=4,'rows_2'=8,'sub'=2] {'rows_0','rows_1'}, dimensions={0} | all-to-all | bytes 1179648 | tf_op jit(solution)/shard_map/all_to_all | solution.py:36
  335.2 0.1 reduce_sum.59
  335.3 0.1 copy.40
  335.4 0.1 copy.41
  335.5 8.8 %cholesky.55 = f32[96,96]{1,0:T(8,128)S(1)} custom-call(f32[96,96]{1,0:T(8,128)S(1)} %fusion.5), custom_call_target="Cholesky" | custom-call | tf_op jit(solution)/shard_map/jit(cholesky)/cholesky | solution.py:130
  344.3 0.6 compare_reduce_fusion
  345.0 0.7 fusion.1
  345.6 7.4 %custom-call.11 = f32[1,96,96]{1,2,0:T(8,128)S(1)} custom-call(f32[1,96,96]{2,1,0:T(8,128)S(1)} %fusion.1), custom_call_target="InvertDiagBlocksLowerTriangular" | custom-call | tf_op jit(solution)/shard_map/triangular_solve | solution.py:78
  353.0 0.0 copy-done.5
  353.0 0.8 fusion.3
  353.8 0.8 convolution_multiply_fusion
  (8 shorter events, 0.1 us)
Async XLA Ops:
  0.6 1.3 copy-start
  195.9 1.7 copy-start.1
  200.4 23.8 %copy-start.2 = (bf16[64,6144]{1,0:T(8,128)(2,1)S(1)}, bf16[64,6144]{1,0:T(8,128)(2,1)}, u32[]{:S(2)}) copy-start(bf16[64,6144]{1,0:T(8,128)(2,1)} %param.3) | copy-start | bytes 2359300
  223.2 1.0 copy-start.3
  224.8 0.6 copy-start.4
  260.3 29.7 %all-to-all-start.5 = ((f32[64,24,96]{2,1,0:T(8,128)}), f32[64,24,96]{2,1,0:T(8,128)S(1)}, u32[]{:S(2)}, u32[]{:S(2)}) async-start(f32[64,24,96]{2,1,0:T(8,128)} %bitcast.10), calls=%async_computation.5 | async-start | bytes 1572864 | tf_op jit(solution)/shard_map/all_to_all | solution.py:17
  318.6 34.4 %copy-start.5 = (f32[96,64]{0,1:T(8,128)S(1)}, f32[96,64]{0,1:T(8,128)}, u32[]{:S(2)}) copy-start(f32[96,64]{0,1:T(8,128)} %copy-done.4) | copy-start | bytes 73732
where the time goes:
time: 355 us
  blocking collectives  259 us (73%)
  other arithmetic  38.3 us (11%)
  waiting for transfers between devices  22.9 us (6%)
  matrix products  14.6 us (4%)
  local copies, waits for them, and re-layouts  12.2 us (3%)
  starting transfers between devices  6.75 us (2%)
    all_to_all x4, blocking collectives, from_everyone(): return lax.all_to_all(copies, axis, split_axis=0, concat_axis=0, tiled=True)  133 us
    all_to_all x2, blocking collectives, sent_and_summed(): lax.all_to_all(in_blocks(array, dim, devices), axis, 0, 0, tiled=True)  118 us
    all_to_all x1, waiting for transfers between devices, sent_and_summed(): lax.all_to_all(in_blocks(array, dim, devices), axis, 0, 0, tiled=True)  22.9 us
    another operation x4, other arithmetic, solve_right(): lax.linalg.triangular_solve(factor, matrix, left_side=False, lower=True,...  16 us
    another operation x3, other arithmetic, on_device(): jnp.linalg.cholesky(gram_one)  9.45 us
    another operation x3, other arithmetic, on_device(): factor_two = jnp.linalg.cholesky(gram_two)  9.45 us
    all_to_all x1, blocking collectives, sum_in_two_steps(): return jnp.sum(lax.all_to_all(own, far, 0, 0, tiled=True), axis=0)  8.2 us
  transfers between devices with their start and end apart: 1, of which 1 were waited for; matrix products, arithmetic and copies ran while one was open for 0% of the time, Pallas kernels for 0%

commit v1 on v0

v1 whole, which is shorter than its diff:
```python
import jax
import jax.numpy as jnp
from jax import lax
from jax.sharding import Mesh
from jax.sharding import PartitionSpec as P

PLANE = ("x", "y")
LINE = ("z", "core")
EVERY = ("x", "y", "z", "core")


def exchanged(array, axes):
    return lax.all_to_all(array, axes, 0, 0, tiled=True)


def from_everyone(array, axes):
    return exchanged(jnp.broadcast_to(array, (lax.axis_size(axes), *array.shape)), axes)


def solve_right(factor, matrix):
    return lax.linalg.triangular_solve(
        factor, matrix, left_side=False, lower=True, transpose_a=True
    )


def over_tokens(left, right):
    return lax.dot_general(
        left, right, (((0,), (0,)), ((), ())), preferred_element_type=jnp.float32
    )


def in_two(array):
    high = lax.reduce_precision(array, 8, 7)
    return high.astype(jnp.bfloat16), (array - high).astype(jnp.bfloat16)


def gram_of(high, low, total):
    product = over_tokens(high, high) + over_tokens(low, high)
    return (product + product.T) / (2.0 * total)


def on_device(tokens_x, test_matrix):
    rows, width = tokens_x.shape
    columns = test_matrix.shape[0]
    plane, line, pair = (lax.axis_size(a) for a in (PLANE, LINE, "core"))
    total = jnp.float32(rows * plane * line)
    block = width // plane
    share = block // line
    sketch = lax.dot_general(
        tokens_x, test_matrix, (((1,), (1,)), ((), ())), preferred_element_type=jnp.float32
    )
    high, low = in_two(sketch)
    blocks = jnp.swapaxes(tokens_x.reshape(rows, plane, block), 0, 1)
    both = jnp.broadcast_to(jnp.concatenate([high, low], 1), (plane, rows, 2 * columns))
    mixed = exchanged(jnp.concatenate([blocks, both], 2), PLANE).reshape(plane * rows, -1)
    tokens = mixed[:, :block]
    high = mixed[:, block : block + columns]
    low = mixed[:, block + columns :]
    gram = gram_of(high, low, total)
    cross = over_tokens(tokens, high)
    sent = jnp.concatenate(
        [cross.reshape(line, share, columns), gram.reshape(line, -1, columns)], 1
    )
    whole = from_everyone(jnp.sum(exchanged(sent, LINE), 0), LINE)
    cross = whole[:, :share].reshape(block, columns)
    gram_one = whole[:, share:].reshape(columns, columns)
    middle = solve_right(jnp.linalg.cholesky(gram_one), cross).astype(jnp.bfloat16)
    power = jnp.dot(tokens, middle, preferred_element_type=jnp.float32)
    power = jnp.sum(exchanged(power.reshape(plane, rows, columns), PLANE), 0)
    powers = from_everyone(power, PLANE).reshape(plane * rows, columns)
    high, low = in_two(powers)
    gram = gram_of(high, low, total)
    cross_two = over_tokens(tokens, high)
    halves = jnp.broadcast_to(
        gram.reshape(1, pair, -1, columns), (line // pair, pair, columns // pair, columns)
    )
    sent = jnp.concatenate(
        [cross_two.reshape(line, share, columns), halves.reshape(line, -1, columns)], 1
    )
    own = jnp.sum(exchanged(sent, LINE), 0)
    cross_two = own[:share]
    gram_two = lax.all_gather(own[share:], "core", axis=0, tiled=True)
    factor_two = jnp.linalg.cholesky(gram_two)
    basis = solve_right(factor_two, power)
    projected = solve_right(factor_two, cross_two) / jnp.sqrt(total)
    return (basis, projected)


def solution(mesh):
    finer = Mesh(mesh.devices.reshape(4, 4, 8, mesh.shape["sub"]), EVERY)
    return jax.shard_map(
        on_device,
        mesh=finer,
        in_specs=(P(EVERY, None), P()),
        out_specs=(P(EVERY, None), P(EVERY, None)),
        check_vma=False,
    )
```

time: 355 us -> 162 us (0.46)
  blocking collectives: 259 us -> 103 us
  waiting for transfers between devices: 22.9 us -> 7.54 us
  matrix products: 14.6 us -> 5.91 us
  local copies, waits for them, and re-layouts: 12.2 us -> 5.05 us
    all_to_all x7 -> x5, blocking collectives: 259 us -> 101 us  [exchanged(): return lax.all_to_all(array, axes, 0, 0, tiled=True)]
    all_to_all x1, waiting for transfers between devices: 22.9 us -> 7.54 us  [exchanged(): return lax.all_to_all(array, axes, 0, 0, tiled=True)]
    another operation x3, matrix products: 6.86 us -> 1.98 us  [solve_right(): lax.linalg.triangular_solve(factor, matrix, left_side=False, lower=True,...]
    dot_general x5 -> x8, matrix products: 7.75 us -> 3.93 us  [the longest x6 1.9 us: over_tokens(): lax.dot_general(left, right, (((0,), (0,)), ((), ())), preferred_element_...]
  transfers between devices with their start and end apart: 1 -> 1, of which waited for: 1 -> 1; matrix products, arithmetic and copies ran while one was open for 0% -> 1% of each run, Pallas kernels for 0% -> 0%
where the time goes in v1:
time: 162 us; the launch traced here: 161 us
  blocking collectives  103 us (64%)
  other arithmetic  35.4 us (22%)
  waiting for transfers between devices  7.54 us (5%)
  matrix products  5.91 us (4%)
  local copies, waits for them, and re-layouts  5.05 us (3%)
  starting transfers between devices  3.64 us (2%)
    all_to_all x5, blocking collectives, exchanged(): return lax.all_to_all(array, axes, 0, 0, tiled=True)  101 us
    another operation x4, other arithmetic, solve_right(): lax.linalg.triangular_solve(factor, matrix, left_side=False, lower=True,...  16 us
    another operation x3, other arithmetic, on_device(): factor_two = jnp.linalg.cholesky(gram_two)  9.45 us
    another operation x3, other arithmetic, on_device(): jnp.linalg.cholesky(gram_one)  9.45 us
    all_to_all x1, waiting for transfers between devices, exchanged(): return lax.all_to_all(array, axes, 0, 0, tiled=True)  7.54 us
    all_to_all x1, starting transfers between devices, exchanged(): return lax.all_to_all(array, axes, 0, 0, tiled=True)  3.64 us
  transfers between devices with their start and end apart: 1, of which 1 were waited for; matrix products, arithmetic and copies ran while one was open for 1% of the time, Pallas kernels for 0%

profile of v1, /device:TPU:1, one launch (start us, length us, event | category | flops | bytes accessed | tf_op | source)
XLA Modules:
  0.0 161.1 jit_solution(17615759027861024929)
XLA Ops:
  0.6 0.0 copy-start
  0.6 0.0 copy-start.1
  0.7 1.3 copy-done
  1.9 1.7 %reduce-precision_convert_fusion.1 = (bf16[64,96]{1,0:T(8,128)(2,1)S(1)}, bf16[64,96]{1,0:T(8,128)(2,1)S(1)}) fusion(bf16[64,6144]{1,0:T(8,128)(2,1)} %param.3, bf16[96,6144]{1,0:T(8,128)(2,1)S(1)} %copy-done), kind=kOutput, calls=%fused_computation.44 | convolution fusion | flops 75522048 | bytes 1990656 | tf_op jit(solution)/shard_map/dot_general | solution.py:49
  3.6 0.0 copy-done.1
  3.6 0.1 copy.56
  3.7 0.1 pad_maximum_fusion.3
  3.9 0.2 pad_maximum_fusion
  4.0 26.3 %all_to_all.30 = bf16[16,64,576]{2,1,0:T(8,128)(2,1)S(1)} all-to-all(bf16[16,64,576]{2,1,0:T(8,128)(2,1)S(1)} %pad_maximum_fusion), channel_id=1, replica_groups=mesh['x'=4,'y'=4,'z'=8,'core'=2] {'x','y'}, dimensions={0} | all-to-all | bytes 2359296 | tf_op jit(solution)/shard_map/all_to_all | solution.py:13
  30.4 0.2 fusion.9
  30.6 0.4 fusion.3
  31.0 0.3 convolution_add_fusion
  31.4 0.1 copy.37
  31.5 21.6 %all_to_all.31 = f32[16,30,96]{2,1,0:T(8,128)S(1)} all-to-all(f32[16,30,96]{2,1,0:T(8,128)S(1)} %pad_maximum_fusion.2), channel_id=1, replica_groups=mesh['x'=4,'y'=4,'z'=8,'core'=2] {'z','core'}, dimensions={0} | all-to-all | bytes 368640 | tf_op jit(solution)/shard_map/all_to_all | solution.py:13
  53.2 14.4 %all_to_all.32 = f32[16,30,96]{2,1,0:T(8,128)S(1)} all-to-all(f32[16,30,96]{2,1,0:T(8,128)S(1)} %broadcast_in_dim.18), channel_id=1, replica_groups=mesh['x'=4,'y'=4,'z'=8,'core'=2] {'z','core'}, dimensions={0} | all-to-all | bytes 368640 | tf_op jit(solution)/shard_map/all_to_all | solution.py:13
  67.6 0.1 copy.38
  67.7 8.8 %cholesky.44 = f32[96,96]{1,0:T(8,128)S(1)} custom-call(f32[96,96]{1,0:T(8,128)S(1)} %fusion.20), custom_call_target="Cholesky" | custom-call | tf_op jit(solution)/shard_map/jit(cholesky)/cholesky | solution.py:67
  76.5 0.6 compare_reduce_fusion.1
  77.1 0.7 fusion.12
  77.8 7.4 %custom-call.10 = f32[1,96,96]{1,2,0:T(8,128)S(1)} custom-call(f32[1,96,96]{2,1,0:T(8,128)S(1)} %fusion.12), custom_call_target="InvertDiagBlocksLowerTriangular" | custom-call | tf_op jit(solution)/shard_map/triangular_solve | solution.py:21
  85.2 0.4 convolution_convert_fusion
  85.6 0.4 fusion.1
  86.0 14.3 %all_to_all.33 = f32[16,64,96]{2,1,0:T(8,128)S(1)} all-to-all(f32[16,64,96]{2,1,0:T(8,128)S(1)} %bitcast.72), channel_id=1, replica_groups=mesh['x'=4,'y'=4,'z'=8,'core'=2] {'x','y'}, dimensions={0} | all-to-all | bytes 786432 | tf_op jit(solution)/shard_map/all_to_all | solution.py:13
  100.3 0.9 broadcast_in_dim.19
  101.2 3.6 %all-to-all-start.4 = ((f32[16,64,96]{2,1,0:T(8,128)}), f32[16,64,96]{2,1,0:T(8,128)S(1)}, u32[]{:S(2)}, u32[]{:S(2)}) async-start(f32[16,64,96]{2,1,0:T(8,128)} %broadcast_in_dim.19), calls=%async_computation.4 | async-start | bytes 1048576 | tf_op jit(solution)/shard_map/all_to_all | solution.py:13
  104.8 1.0 slice_bitcast_fusion
  105.8 1.4 copy.40
  107.2 7.5 %all-to-all-done.4 = f32[16,64,96]{2,1,0:T(8,128)S(1)} async-done(((f32[16,64,96]{2,1,0:T(8,128)}), f32[16,64,96]{2,1,0:T(8,128)S(1)}, u32[]{:S(2)}, u32[]{:S(2)}) %all-to-all-start.4) | async-done | bytes 393248 | tf_op jit(solution)/shard_map/all_to_all | solution.py:13
  114.8 0.3 convolution_bitcast_fusion.1
  115.0 0.3 fusion
  115.3 0.1 copy.44
  115.4 0.4 fusion.24
  115.9 24.0 %all_to_all.34 = f32[16,72,96]{2,1,0:T(8,128)S(1)} all-to-all(f32[16,72,96]{2,1,0:T(8,128)S(1)} %pad_maximum_fusion.1), channel_id=1, replica_groups=mesh['x'=4,'y'=4,'z'=8,'core'=2] {'z','core'}, dimensions={0} | all-to-all | bytes 884736 | tf_op jit(solution)/shard_map/all_to_all | solution.py:13
  139.9 0.1 reduce_sum.29
  140.0 2.0 %all_gather.3 = f32[96,96]{1,0:T(8,128)S(1)} all-gather(f32[48,96]{1,0:T(8,128)S(1)} %slice.47), channel_id=1, replica_groups=mesh['x'=4,'y'=4,'z'=8,'core'=2] {'core'}, dimensions={0}, use_global_device_ids=true | all-gather | bytes 55296 | tf_op jit(solution)/shard_map/all_gather | solution.py:82
  142.0 0.1 copy.45
  142.1 8.8 %cholesky.55 = f32[96,96]{1,0:T(8,128)S(1)} custom-call(f32[96,96]{1,0:T(8,128)S(1)} %fusion.17), custom_call_target="Cholesky" | custom-call | tf_op jit(solution)/shard_map/jit(cholesky)/cholesky | solution.py:83
  150.9 0.6 compare_reduce_fusion
  151.6 0.7 fusion.13
  152.2 7.4 %custom-call.11 = f32[1,96,96]{1,2,0:T(8,128)S(1)} custom-call(f32[1,96,96]{2,1,0:T(8,128)S(1)} %fusion.13), custom_call_target="InvertDiagBlocksLowerTriangular" | custom-call | tf_op jit(solution)/shard_map/triangular_solve | solution.py:21
  159.6 0.8 convolution_multiply_fusion
  160.3 0.8 fusion.15
  (19 shorter events, 0.4 us)
Async XLA Ops:
  0.6 1.3 copy-start
  0.6 2.9 %copy-start.1 = (bf16[64,6144]{1,0:T(8,128)(2,1)S(1)}, bf16[64,6144]{1,0:T(8,128)(2,1)}, u32[]{:S(2)}) copy-start(bf16[64,6144]{1,0:T(8,128)(2,1)} %param.3) | copy-start | bytes 2359300
  101.2 13.6 %all-to-all-start.4 = ((f32[16,64,96]{2,1,0:T(8,128)}), f32[16,64,96]{2,1,0:T(8,128)S(1)}, u32[]{:S(2)}, u32[]{:S(2)}) async-start(f32[16,64,96]{2,1,0:T(8,128)} %broadcast_in_dim.19), calls=%async_computation.4 | async-start | bytes 1048576 | tf_op jit(solution)/shard_map/all_to_all | solution.py:13

commit v2 on v1

--- a/solution.py
+++ b/solution.py
@@ -1,12 +1,14 @@
 import jax
 import jax.numpy as jnp
 from jax import lax
+from jax.experimental import pallas as pl
 from jax.sharding import Mesh
 from jax.sharding import PartitionSpec as P
 
 PLANE = ("x", "y")
 LINE = ("z", "core")
 EVERY = ("x", "y", "z", "core")
+GROUP = 8
 
 
 def exchanged(array, axes):
@@ -17,9 +19,65 @@
     return exchanged(jnp.broadcast_to(array, (lax.axis_size(axes), *array.shape)), axes)
 
 
-def solve_right(factor, matrix):
-    return lax.linalg.triangular_solve(
-        factor, matrix, left_side=False, lower=True, transpose_a=True
+def inverse_factor_kernel(gram, inverse):
+    size = gram.shape[0]
+    shape = (GROUP, size)
+    lane = lax.broadcasted_iota(jnp.int32, shape, 1)
+    row = lax.broadcasted_iota(jnp.int32, shape, 0)
+
+    def column(value, at):
+        return jnp.broadcast_to(value[:, at : at + 1], shape)
+
+    def line(value, at):
+        return jnp.broadcast_to(value[at : at + 1], shape)
+
+    groups = [gram[pl.ds(first, GROUP), :] for first in range(0, size, GROUP)]
+    for at, own in enumerate(groups):
+        first = at * GROUP
+        columns = [column(own, first + k) for k in range(GROUP)]
+        pivots = jnp.ones(shape, jnp.float32)
+        lines, scales, uppers = [], [], {}
+        for k in range(GROUP):
+            pivot = line(columns[k], k)
+            scale = 1.0 / pivot
+            pivots = jnp.where(row == k, pivot, pivots)
+            factor = jnp.where(row > k, columns[k] * scale, 0.0)
+            own = jnp.where((lane == first + k) & (row >= k), jnp.where(row == k, 1.0, 0.0), own)
+            lines.append(line(own, k))
+            scales.append(scale)
+            own = own - factor * lines[k]
+            lines[k] = jnp.where((lane > first + k) & (lane < first + GROUP), 0.0, lines[k])
+            for j in range(k + 1, GROUP):
+                uppers[k, j] = line(columns[j], k)
+                columns[j] = columns[j] - factor * uppers[k, j]
+        inverse[pl.ds(first, GROUP), :] = jnp.where(
+            lane <= first + row, own * lax.rsqrt(pivots), 0.0
+        )
+        inside = (lane >= first) & (lane < first + GROUP)
+        for later in range(at + 1, len(groups)):
+            value = groups[later]
+            columns = [column(value, first + k) for k in range(GROUP)]
+            value = jnp.where(inside, 0.0, value)
+            for k in range(GROUP):
+                factor = columns[k] * scales[k]
+                value = value - factor * lines[k]
+                for j in range(k + 1, GROUP):
+                    columns[j] = columns[j] - factor * uppers[k, j]
+            groups[later] = value
+
+def inverse_factor(gram):
+    return pl.pallas_call(
+        inverse_factor_kernel, out_shape=jax.ShapeDtypeStruct(gram.shape, jnp.float32)
+    )(gram)
+
+
+def solved(matrix, inverse):
+    return lax.dot_general(
+        matrix,
+        inverse,
+        (((1,), (1,)), ((), ())),
+        precision=lax.Precision.HIGHEST,
+        preferred_element_type=jnp.float32,
     )
 
 
@@ -58,13 +116,18 @@
     low = mixed[:, block + columns :]
     gram = gram_of(high, low, total)
     cross = over_tokens(tokens, high)
+    part = columns // line
     sent = jnp.concatenate(
-        [cross.reshape(line, share, columns), gram.reshape(line, -1, columns)], 1
+        [
+            cross.reshape(line, share, columns),
+            jnp.pad(gram.reshape(line, part, columns), ((0, 0), (0, GROUP - part), (0, 0))),
+        ],
+        1,
     )
     whole = from_everyone(jnp.sum(exchanged(sent, LINE), 0), LINE)
     cross = whole[:, :share].reshape(block, columns)
-    gram_one = whole[:, share:].reshape(columns, columns)
-    middle = solve_right(jnp.linalg.cholesky(gram_one), cross).astype(jnp.bfloat16)
+    gram_one = whole[:, share : share + part].reshape(columns, columns)
+    middle = solved(cross, inverse_factor(gram_one)).astype(jnp.bfloat16)
     power = jnp.dot(tokens, middle, preferred_element_type=jnp.float32)
     power = jnp.sum(exchanged(power.reshape(plane, rows, columns), PLANE), 0)
     powers = from_everyone(power, PLANE).reshape(plane * rows, columns)
@@ -80,9 +143,9 @@
     own = jnp.sum(exchanged(sent, LINE), 0)
     cross_two = own[:share]
     gram_two = lax.all_gather(own[share:], "core", axis=0, tiled=True)
-    factor_two = jnp.linalg.cholesky(gram_two)
-    basis = solve_right(factor_two, power)
-    projected = solve_right(factor_two, cross_two) / jnp.sqrt(total)
+    inverse_two = inverse_factor(gram_two)
+    basis = solved(power, inverse_two)
+    projected = solved(cross_two, inverse_two) / jnp.sqrt(total)
     return (basis, projected)
 
 

time: 162 us -> 138 us (0.85)
  other arithmetic: 35.4 us -> 0.5 us
  Pallas kernels: 0 us -> 8.46 us
  matrix products: 5.91 us -> 8.36 us
    another operation x10 -> x0, other arithmetic: 34.9 us -> none  [the longest x4 16 us: solve_right(): lax.linalg.triangular_solve(factor, matrix, left_side=False, lower=True,...]
    pallas_call x0 -> x2, Pallas kernels: none -> 8.46 us  [inverse_factor(): pl.pallas_call(inverse_factor_kernel, out_shape=jax.ShapeDtypeStruct(gram...]
    dot_general x0 -> x3, matrix products: none -> 4.42 us  [solved(): lax.dot_general(matrix, inverse, (((1,), (1,)), ((), ())), precision=lax....]
    another operation x3 -> x0, matrix products: 1.98 us -> none  [solve_right(): lax.linalg.triangular_solve(factor, matrix, left_side=False, lower=True,...]
  transfers between devices with their start and end apart: 1 -> 1, of which waited for: 1 -> 1; matrix products, arithmetic and copies ran while one was open for 1% -> 2% of each run, Pallas kernels for 0% -> 0%
where the time goes in v2:
time: 138 us; the launch traced here: 137 us
  blocking collectives  102 us (74%)
  Pallas kernels  8.46 us (6%)
  matrix products  8.36 us (6%)
  waiting for transfers between devices  7.54 us (5%)
  local copies, waits for them, and re-layouts  5.51 us (4%)
  starting transfers between devices  4.03 us (3%)
    all_to_all x5, blocking collectives, exchanged(): return lax.all_to_all(array, axes, 0, 0, tiled=True)  100 us
    pallas_call x2, Pallas kernels, inverse_factor(): pl.pallas_call(inverse_factor_kernel, out_shape=jax.ShapeDtypeStruct(gram...  8.46 us
    all_to_all x1, waiting for transfers between devices, exchanged(): return lax.all_to_all(array, axes, 0, 0, tiled=True)  7.54 us
    dot_general x3, matrix products, solved(): lax.dot_general(matrix, inverse, (((1,), (1,)), ((), ())), precision=lax....  4.42 us
    all_to_all x1, starting transfers between devices, exchanged(): return lax.all_to_all(array, axes, 0, 0, tiled=True)  4.03 us
  transfers between devices with their start and end apart: 1, of which 1 were waited for; matrix products, arithmetic and copies ran while one was open for 2% of the time, Pallas kernels for 0%

profile of v2, /device:TPU:1, one launch (start us, length us, event | category | flops | bytes accessed | tf_op | source)
XLA Modules:
  0.0 137.4 jit_solution(1616673427078114982)
XLA Ops:
  0.6 0.0 copy-start
  0.6 0.0 copy-start.1
  0.7 1.3 copy-done
  1.9 1.7 %reduce-precision_convert_fusion.1 = (bf16[64,96]{1,0:T(8,128)(2,1)S(1)}, bf16[64,96]{1,0:T(8,128)(2,1)S(1)}) fusion(bf16[64,6144]{1,0:T(8,128)(2,1)} %param.2, bf16[96,6144]{1,0:T(8,128)(2,1)S(1)} %copy-done), kind=kOutput, calls=%fused_computation.29 | convolution fusion | flops 75522048 | bytes 1990656 | tf_op jit(solution)/shard_map/dot_general | solution.py:107
  3.6 0.0 copy-done.1
  3.6 0.1 copy.39
  3.7 0.1 pad_maximum_fusion.2
  3.9 0.2 pad_maximum_fusion
  4.0 26.3 %all_to_all.30 = bf16[16,64,576]{2,1,0:T(8,128)(2,1)S(1)} all-to-all(bf16[16,64,576]{2,1,0:T(8,128)(2,1)S(1)} %pad_maximum_fusion), channel_id=1, replica_groups=mesh['x'=4,'y'=4,'z'=8,'core'=2] {'x','y'}, dimensions={0} | all-to-all | bytes 2359296 | tf_op jit(solution)/shard_map/all_to_all | solution.py:15
  30.4 0.2 fusion.9
  30.6 0.4 fusion.3
  31.0 0.3 convolution_add_fusion
  31.4 0.1 copy.22
  31.5 21.6 %all_to_all.31 = f32[16,32,96]{2,1,0:T(8,128)S(1)} all-to-all(f32[16,32,96]{2,1,0:T(8,128)S(1)} %select_maximum_fusion), channel_id=1, replica_groups=mesh['x'=4,'y'=4,'z'=8,'core'=2] {'z','core'}, dimensions={0} | all-to-all | bytes 393216 | tf_op jit(solution)/shard_map/all_to_all | solution.py:15
  53.2 14.4 %all_to_all.32 = f32[16,32,96]{2,1,0:T(8,128)S(1)} all-to-all(f32[16,32,96]{2,1,0:T(8,128)S(1)} %broadcast_in_dim.17), channel_id=1, replica_groups=mesh['x'=4,'y'=4,'z'=8,'core'=2] {'z','core'}, dimensions={0} | all-to-all | bytes 393216 | tf_op jit(solution)/shard_map/all_to_all | solution.py:15
  67.6 0.6 reshape.43.gram
  68.2 4.2 %shard_map.41 = f32[96,96]{1,0:T(8,128)} custom-call(f32[96,96]{1,0:T(8,128)} %reshape.43.gram), custom_call_target="tpu_custom_call" | custom-call | tf_op jit(solution)/shard_map/pallas_call | solution.py:69
  72.4 1.2 convolution_convert_fusion
  73.6 0.4 fusion.1
  74.0 13.9 %all_to_all.33 = f32[16,64,96]{2,1,0:T(8,128)S(1)} all-to-all(f32[16,64,96]{2,1,0:T(8,128)S(1)} %bitcast.55), channel_id=1, replica_groups=mesh['x'=4,'y'=4,'z'=8,'core'=2] {'x','y'}, dimensions={0} | all-to-all | bytes 786432 | tf_op jit(solution)/shard_map/all_to_all | solution.py:15
  88.0 0.9 broadcast_in_dim.18
  88.8 4.0 %all-to-all-start.4 = ((f32[16,64,96]{2,1,0:T(8,128)}), f32[16,64,96]{2,1,0:T(8,128)S(1)}, u32[]{:S(2)}, u32[]{:S(2)}) async-start(f32[16,64,96]{2,1,0:T(8,128)} %broadcast_in_dim.18), calls=%async_computation.4 | async-start | bytes 1048576 | tf_op jit(solution)/shard_map/all_to_all | solution.py:15
  92.8 1.0 slice_bitcast_fusion
  93.8 1.4 %copy.24 = bf16[384,1024]{1,0:T(8,128)(2,1)S(1)} copy(bf16[384,1024]{0,1:T(8,128)(2,1)} %slice_bitcast_fusion) | data formatting | bytes 1572864 | tf_op jit(solution)/shard_map/dot_general | solution.py:85
  95.2 7.5 %all-to-all-done.4 = f32[16,64,96]{2,1,0:T(8,128)S(1)} async-done(((f32[16,64,96]{2,1,0:T(8,128)}), f32[16,64,96]{2,1,0:T(8,128)S(1)}, u32[]{:S(2)}, u32[]{:S(2)}) %all-to-all-start.4) | async-done | bytes 393248 | tf_op jit(solution)/shard_map/all_to_all | solution.py:15
  102.8 0.3 convolution_bitcast_fusion.1
  103.1 0.3 fusion
  103.3 0.1 copy.28
  103.4 0.4 fusion.16
  103.9 24.0 %all_to_all.34 = f32[16,72,96]{2,1,0:T(8,128)S(1)} all-to-all(f32[16,72,96]{2,1,0:T(8,128)S(1)} %pad_maximum_fusion.1), channel_id=1, replica_groups=mesh['x'=4,'y'=4,'z'=8,'core'=2] {'z','core'}, dimensions={0} | all-to-all | bytes 884736 | tf_op jit(solution)/shard_map/all_to_all | solution.py:15
  127.9 0.1 reduce_sum.29
  128.0 2.0 %all_gather.3.gram = f32[96,96]{1,0:T(8,128)} all-gather(f32[48,96]{1,0:T(8,128)S(1)} %slice.33), channel_id=1, replica_groups=mesh['x'=4,'y'=4,'z'=8,'core'=2] {'core'}, dimensions={0}, use_global_device_ids=true | all-gather | bytes 55296 | tf_op jit(solution)/shard_map/all_gather | solution.py:145
  130.0 4.2 %shard_map.42 = f32[96,96]{1,0:T(8,128)} custom-call(f32[96,96]{1,0:T(8,128)} %all_gather.3.gram), custom_call_target="tpu_custom_call" | custom-call | tf_op jit(solution)/shard_map/pallas_call | solution.py:69
  134.2 1.6 %convolution_multiply_fusion = f32[24,96]{1,0:T(8,128)} fusion(f32[96,96]{1,0:T(8,128)} %shard_map.42, f32[72,96]{1,0:T(8,128)S(1)} %reduce_sum.29), kind=kOutput, calls=%fused_computation.6 | convolution fusion | flops 2656512 | bytes 58368 | tf_op jit(solution)/shard_map/dot_general | solution.py:75
  135.8 1.6 %fusion.17 = f32[64,96]{1,0:T(8,128)} fusion(f32[64,96]{1,0:T(8,128)S(1)} %reduce_sum.28, f32[96,96]{1,0:T(8,128)} %shard_map.42), kind=kOutput, calls=%fused_computation.34 | convolution fusion | flops 7077888 | bytes 86016 | tf_op jit(solution)/shard_map/dot_general | solution.py:75
  (14 shorter events, 0.3 us)
Async XLA Ops:
  0.6 1.3 copy-start
  0.6 2.9 %copy-start.1 = (bf16[64,6144]{1,0:T(8,128)(2,1)S(1)}, bf16[64,6144]{1,0:T(8,128)(2,1)}, u32[]{:S(2)}) copy-start(bf16[64,6144]{1,0:T(8,128)(2,1)} %param.2) | copy-start | bytes 2359300
  88.8 13.9 %all-to-all-start.4 = ((f32[16,64,96]{2,1,0:T(8,128)}), f32[16,64,96]{2,1,0:T(8,128)S(1)}, u32[]{:S(2)}, u32[]{:S(2)}) async-start(f32[16,64,96]{2,1,0:T(8,128)} %broadcast_in_dim.18), calls=%async_computation.4 | async-start | bytes 1048576 | tf_op jit(solution)/shard_map/all_to_all | solution.py:15

commit v3 on v2

--- a/solution.py
+++ b/solution.py
@@ -9,6 +9,7 @@
 LINE = ("z", "core")
 EVERY = ("x", "y", "z", "core")
 GROUP = 8
+LANES = 128
 
 
 def exchanged(array, axes):
@@ -109,11 +110,13 @@
     )
     high, low = in_two(sketch)
     blocks = jnp.swapaxes(tokens_x.reshape(rows, plane, block), 0, 1)
-    both = jnp.broadcast_to(jnp.concatenate([high, low], 1), (plane, rows, 2 * columns))
-    mixed = exchanged(jnp.concatenate([blocks, both], 2), PLANE).reshape(plane * rows, -1)
+    spare = -(block + 2 * columns) % LANES
+    own = jnp.pad(jnp.concatenate([high, low], 1), ((0, 0), (0, spare)))
+    own = jnp.broadcast_to(own, (plane, *own.shape))
+    mixed = exchanged(jnp.concatenate([blocks, own], 2), PLANE).reshape(plane * rows, -1)
     tokens = mixed[:, :block]
     high = mixed[:, block : block + columns]
-    low = mixed[:, block + columns :]
+    low = mixed[:, block + columns : block + 2 * columns]
     gram = gram_of(high, low, total)
     cross = over_tokens(tokens, high)
     part = columns // line
@@ -134,13 +137,15 @@
     high, low = in_two(powers)
     gram = gram_of(high, low, total)
     cross_two = over_tokens(tokens, high)
-    halves = jnp.broadcast_to(
-        gram.reshape(1, pair, -1, columns), (line // pair, pair, columns // pair, columns)
-    )
-    sent = jnp.concatenate(
-        [cross_two.reshape(line, share, columns), halves.reshape(line, -1, columns)], 1
-    )
-    own = jnp.sum(exchanged(sent, LINE), 0)
+    own = lax.axis_index("core")
+    both = lax.all_gather(jnp.concatenate([cross_two, gram]), "core")
+    both = both[0] + both[1]
+    lines = both[:block].reshape(line // pair, pair, share, columns)
+    half = both[block:].reshape(pair, -1, columns)
+    lines = lax.dynamic_index_in_dim(lines, own, 1, False)
+    half = lax.dynamic_index_in_dim(half, own, 0, False)
+    half = jnp.broadcast_to(half, (line // pair, *half.shape))
+    own = jnp.sum(exchanged(jnp.concatenate([lines, half], 1), "z"), 0)
     cross_two = own[:share]
     gram_two = lax.all_gather(own[share:], "core", axis=0, tiled=True)
     inverse_two = inverse_factor(gram_two)

time: 138 us -> 135 us (0.978)
  blocking collectives: 102 us -> 98.4 us
  waiting for transfers between devices: 7.54 us -> 9.9 us
  local copies, waits for them, and re-layouts: 5.51 us -> 3.8 us
    all_to_all x5, blocking collectives: 100 us -> 91.6 us  [exchanged(): return lax.all_to_all(array, axes, 0, 0, tiled=True)]
    all_gather x0 -> x1, blocking collectives: none -> 4.26 us  [on_device(): both = lax.all_gather(jnp.concatenate([cross_two, gram]), 'core')]
    all_to_all x1, waiting for transfers between devices: 7.54 us -> 9.9 us  [exchanged(): return lax.all_to_all(array, axes, 0, 0, tiled=True)]
    dot_general x2 -> x0, local copies, waits for them, and re-layouts: 2.36 us -> none  [over_tokens(): lax.dot_general(left, right, (((0,), (0,)), ((), ())), preferred_element_...]
  transfers between devices with their start and end apart: 1 -> 1, of which waited for: 1 -> 1; matrix products, arithmetic and copies ran while one was open for 2% -> 0% of each run, Pallas kernels for 0% -> 0%
where the time goes in v3:
time: 135 us; the launch traced here: 134 us
  blocking collectives  98.4 us (73%)
  waiting for transfers between devices  9.9 us (7%)
  Pallas kernels  8.46 us (6%)
  matrix products  8.29 us (6%)
  local copies, waits for them, and re-layouts  3.8 us (3%)
  starting transfers between devices  3.63 us (3%)
    all_to_all x5, blocking collectives, exchanged(): return lax.all_to_all(array, axes, 0, 0, tiled=True)  91.6 us
    all_to_all x1, waiting for transfers between devices, exchanged(): return lax.all_to_all(array, axes, 0, 0, tiled=True)  9.9 us
    pallas_call x2, Pallas kernels, inverse_factor(): pl.pallas_call(inverse_factor_kernel, out_shape=jax.ShapeDtypeStruct(gram...  8.46 us
    dot_general x3, matrix products, solved(): lax.dot_general(matrix, inverse, (((1,), (1,)), ((), ())), precision=lax....  4.42 us
    all_gather x1, blocking collectives, on_device(): both = lax.all_gather(jnp.concatenate([cross_two, gram]), 'core')  4.26 us
    all_to_all x1, starting transfers between devices, exchanged(): return lax.all_to_all(array, axes, 0, 0, tiled=True)  3.63 us
  transfers between devices with their start and end apart: 1, of which 1 were waited for; matrix products, arithmetic and copies ran while one was open for 0% of the time, Pallas kernels for 0%

profile of v3, /device:TPU:1, one launch (start us, length us, event | category | flops | bytes accessed | tf_op | source)
XLA Modules:
  0.0 133.9 jit_solution(15842127086318732908)
XLA Ops:
  0.6 0.0 copy-start
  0.6 0.0 copy-start.1
  0.7 1.3 copy-done
  1.9 1.7 %reduce-precision_convert_fusion.1 = (bf16[64,96]{1,0:T(8,128)(2,1)S(1)}, bf16[64,96]{1,0:T(8,128)(2,1)S(1)}) fusion(bf16[64,6144]{1,0:T(8,128)(2,1)} %param.2, bf16[96,6144]{1,0:T(8,128)(2,1)S(1)} %copy-done), kind=kOutput, calls=%fused_computation.34 | convolution fusion | flops 75522048 | bytes 1990656 | tf_op jit(solution)/shard_map/dot_general | solution.py:108
  3.6 0.0 copy-done.1
  3.6 0.1 copy.57
  3.7 0.1 fusion.19
  3.9 0.1 pad_maximum_fusion
  4.0 0.3 copy.39
  4.3 26.3 %all_to_all.30 = bf16[16,64,640]{2,1,0:T(8,128)(2,1)S(1)} all-to-all(bf16[16,64,640]{2,1,0:T(8,128)(2,1)S(1)} %copy.39), channel_id=1, replica_groups=mesh['x'=4,'y'=4,'z'=8,'core'=2] {'x','y'}, dimensions={0} | all-to-all | bytes 2621440 | tf_op jit(solution)/shard_map/all_to_all | solution.py:16
  30.6 0.2 fusion.11
  30.9 0.4 fusion.5
  31.3 0.3 convolution_add_fusion
  31.6 0.1 copy.41
  31.8 21.6 %all_to_all.31 = f32[16,32,96]{2,1,0:T(8,128)S(1)} all-to-all(f32[16,32,96]{2,1,0:T(8,128)S(1)} %select_maximum_fusion), channel_id=1, replica_groups=mesh['x'=4,'y'=4,'z'=8,'core'=2] {'z','core'}, dimensions={0} | all-to-all | bytes 393216 | tf_op jit(solution)/shard_map/all_to_all | solution.py:16
  53.4 14.4 %all_to_all.32 = f32[16,32,96]{2,1,0:T(8,128)S(1)} all-to-all(f32[16,32,96]{2,1,0:T(8,128)S(1)} %broadcast_in_dim.13), channel_id=1, replica_groups=mesh['x'=4,'y'=4,'z'=8,'core'=2] {'z','core'}, dimensions={0} | all-to-all | bytes 393216 | tf_op jit(solution)/shard_map/all_to_all | solution.py:16
  67.8 0.6 reshape.48.gram
  68.4 4.2 %shard_map.41 = f32[96,96]{1,0:T(8,128)} custom-call(f32[96,96]{1,0:T(8,128)} %reshape.48.gram), custom_call_target="tpu_custom_call" | custom-call | tf_op jit(solution)/shard_map/pallas_call | solution.py:70
  72.7 1.2 convolution_convert_fusion
  73.9 0.4 fusion.3
  74.3 14.3 %all_to_all.33 = f32[16,64,96]{2,1,0:T(8,128)S(1)} all-to-all(f32[16,64,96]{2,1,0:T(8,128)S(1)} %bitcast.51), channel_id=1, replica_groups=mesh['x'=4,'y'=4,'z'=8,'core'=2] {'x','y'}, dimensions={0} | all-to-all | bytes 786432 | tf_op jit(solution)/shard_map/all_to_all | solution.py:16
  88.6 0.8 broadcast_in_dim.14
  89.5 3.6 %all-to-all-start.4 = ((f32[16,64,96]{2,1,0:T(8,128)}), f32[16,64,96]{2,1,0:T(8,128)S(1)}, u32[]{:S(2)}, u32[]{:S(2)}) async-start(f32[16,64,96]{2,1,0:T(8,128)} %broadcast_in_dim.14), calls=%async_computation.4 | async-start | bytes 1048576 | tf_op jit(solution)/shard_map/all_to_all | solution.py:16
  93.1 9.9 %all-to-all-done.4 = f32[16,64,96]{2,1,0:T(8,128)S(1)} async-done(((f32[16,64,96]{2,1,0:T(8,128)}), f32[16,64,96]{2,1,0:T(8,128)S(1)}, u32[]{:S(2)}, u32[]{:S(2)}) %all-to-all-start.4) | async-done | bytes 393248 | tf_op jit(solution)/shard_map/all_to_all | solution.py:16
  103.1 0.3 convolution_bitcast_fusion.1
  103.3 0.3 fusion
  103.6 0.1 copy.45
  103.7 0.1 copy.46
  103.8 0.3 fusion.1
  104.1 4.3 %all-gather.1 = f32[2,480,96]{1,2,0:T(8,128)S(1)} all-gather(f32[1,480,96]{1,2,0:T(8,128)S(1)} %maximum_bitcast_fusion), channel_id=2, replica_groups=mesh['x'=4,'y'=4,'z'=8,'core'=2] {'core'}, dimensions={0}, use_global_device_ids=true | all-gather | bytes 552960 | tf_op jit(solution)/shard_map/all_gather | solution.py:141
  108.4 0.1 copy.55
  108.5 0.1 copy.56
  108.8 15.0 %all_to_all.34 = f32[8,72,96]{2,1,0:T(8,128)S(1)} all-to-all(f32[8,72,96]{2,1,0:T(8,128)S(1)} %pad_maximum_fusion.1), channel_id=1, replica_groups=mesh['x'=4,'y'=4,'z'=8,'core'=2] {'z'}, dimensions={0} | all-to-all | bytes 442368 | tf_op jit(solution)/shard_map/all_to_all | solution.py:16
  123.9 2.5 %all_gather.11.gram = f32[96,96]{1,0:T(8,128)} all-gather(f32[48,96]{1,0:T(8,128)S(1)} %slice.59), channel_id=1, replica_groups=mesh['x'=4,'y'=4,'z'=8,'core'=2] {'core'}, dimensions={0}, use_global_device_ids=true | all-gather | bytes 55296 | tf_op jit(solution)/shard_map/all_gather | solution.py:150
  126.4 4.2 %shard_map.42 = f32[96,96]{1,0:T(8,128)} custom-call(f32[96,96]{1,0:T(8,128)} %all_gather.11.gram), custom_call_target="tpu_custom_call" | custom-call | tf_op jit(solution)/shard_map/pallas_call | solution.py:70
  130.6 1.6 %convolution_multiply_fusion = f32[24,96]{1,0:T(8,128)} fusion(f32[96,96]{1,0:T(8,128)} %shard_map.42, f32[72,96]{1,0:T(8,128)S(1)} %reduce_sum.29), kind=kOutput, calls=%fused_computation.6 | convolution fusion | flops 2656512 | bytes 58368 | tf_op jit(solution)/shard_map/dot_general | solution.py:76
  132.2 1.6 %fusion.22 = f32[64,96]{1,0:T(8,128)} fusion(f32[64,96]{1,0:T(8,128)S(1)} %reduce_sum.28, f32[96,96]{1,0:T(8,128)} %shard_map.42), kind=kOutput, calls=%fused_computation.40 | convolution fusion | flops 7077888 | bytes 86016 | tf_op jit(solution)/shard_map/dot_general | solution.py:76
  (22 shorter events, 0.5 us)
Async XLA Ops:
  0.6 1.3 copy-start
  0.6 2.9 %copy-start.1 = (bf16[64,6144]{1,0:T(8,128)(2,1)S(1)}, bf16[64,6144]{1,0:T(8,128)(2,1)}, u32[]{:S(2)}) copy-start(bf16[64,6144]{1,0:T(8,128)(2,1)} %param.2) | copy-start | bytes 2359300
  89.5 13.5 %all-to-all-start.4 = ((f32[16,64,96]{2,1,0:T(8,128)}), f32[16,64,96]{2,1,0:T(8,128)S(1)}, u32[]{:S(2)}, u32[]{:S(2)}) async-start(f32[16,64,96]{2,1,0:T(8,128)} %broadcast_in_dim.14), calls=%async_computation.4 | async-start | bytes 1048576 | tf_op jit(solution)/shard_map/all_to_all | solution.py:16

commit v4 on v3

--- a/solution.py
+++ b/solution.py
@@ -1,7 +1,10 @@
+import functools
+
 import jax
 import jax.numpy as jnp
 from jax import lax
 from jax.experimental import pallas as pl
+from jax.experimental.pallas import tpu as pltpu
 from jax.sharding import Mesh
 from jax.sharding import PartitionSpec as P
 
@@ -20,7 +23,7 @@
     return exchanged(jnp.broadcast_to(array, (lax.axis_size(axes), *array.shape)), axes)
 
 
-def inverse_factor_kernel(gram, inverse):
+def invert_factor(gram, inverse):
     size = gram.shape[0]
     shape = (GROUP, size)
     lane = lax.broadcasted_iota(jnp.int32, shape, 1)
@@ -66,20 +69,48 @@
                     columns[j] = columns[j] - factor * uppers[k, j]
             groups[later] = value
 
-def inverse_factor(gram):
-    return pl.pallas_call(
-        inverse_factor_kernel, out_shape=jax.ShapeDtypeStruct(gram.shape, jnp.float32)
-    )(gram)
-
-
-def solved(matrix, inverse):
+def times(left, right, right_dim):
     return lax.dot_general(
-        matrix,
-        inverse,
-        (((1,), (1,)), ((), ())),
+        left,
+        right,
+        (((1,), (right_dim,)), ((), ())),
         precision=lax.Precision.HIGHEST,
         preferred_element_type=jnp.float32,
     )
+
+
+def middle_kernel(gram, cross, middle, inverse):
+    invert_factor(gram, inverse)
+    middle[...] = times(inverse[...], cross[...], 0).astype(jnp.bfloat16)
+
+
+def outputs_kernel(gram, power, cross_two, basis, projected, inverse, *, scale):
+    invert_factor(gram, inverse)
+    basis[...] = times(power[...], inverse[...], 1)
+    projected[...] = times(cross_two[...], inverse[...], 1) * scale
+
+
+def near(*arrays):
+    return [pltpu.with_memory_space_constraint(a, pltpu.VMEM) for a in arrays]
+
+
+def middle_of(gram, cross):
+    return pl.pallas_call(
+        middle_kernel,
+        out_shape=pltpu.VMEM(cross.shape, jnp.bfloat16),
+        scratch_shapes=[pltpu.VMEM(gram.shape, jnp.float32)],
+    )(*near(gram, cross))
+
+
+def outputs_of(gram, power, cross_two, total):
+    return pl.pallas_call(
+        functools.partial(outputs_kernel, scale=float(total) ** -0.5),
+        out_shape=[
+            jax.ShapeDtypeStruct(power.shape, jnp.float32),
+            jax.ShapeDtypeStruct(cross_two.shape, jnp.float32),
+        ],
+        scratch_shapes=[pltpu.VMEM(gram.shape, jnp.float32)],
+    )(*near(gram, power, cross_two))
 
 
 def over_tokens(left, right):
@@ -93,6 +124,13 @@
     return high.astype(jnp.bfloat16), (array - high).astype(jnp.bfloat16)
 
 
+def in_three(array):
+    high = lax.reduce_precision(array, 8, 7)
+    rest = array - high
+    middle = lax.reduce_precision(rest, 8, 7)
+    return [part.astype(jnp.bfloat16) for part in (high, middle, rest - middle)]
+
+
 def gram_of(high, low, total):
     product = over_tokens(high, high) + over_tokens(low, high)
     return (product + product.T) / (2.0 * total)
@@ -102,7 +140,7 @@
     rows, width = tokens_x.shape
     columns = test_matrix.shape[0]
     plane, line, pair = (lax.axis_size(a) for a in (PLANE, LINE, "core"))
-    total = jnp.float32(rows * plane * line)
+    total = rows * plane * line
     block = width // plane
     share = block // line
     sketch = lax.dot_general(
@@ -118,26 +156,26 @@
     high = mixed[:, block : block + columns]
     low = mixed[:, block + columns : block + 2 * columns]
     gram = gram_of(high, low, total)
-    cross = over_tokens(tokens, high)
-    part = columns // line
-    sent = jnp.concatenate(
-        [
-            cross.reshape(line, share, columns),
-            jnp.pad(gram.reshape(line, part, columns), ((0, 0), (0, GROUP - part), (0, 0))),
-        ],
-        1,
+    own = lax.axis_index("core")
+    cross = over_tokens(high, tokens)
+    both = jnp.pad(jnp.concatenate([cross, gram], 1), ((0, 0), (0, -columns % LANES)))
+    both = lax.all_gather(both.reshape(pair, columns // pair, -1), "core")
+    half = lax.dynamic_index_in_dim(both[0] + both[1], own, 0, False)
+    cross = half[:, :block].astype(jnp.bfloat16)
+    sent = from_everyone(jnp.concatenate([cross, *in_three(half[:, block:])], 1), "z")
+    cross = sent[:, :, :block].astype(jnp.float32)
+    gram = sum(part.astype(jnp.float32) for part in jnp.split(sent[:, :, block:], 3, 2))
+    half = jnp.sum(jnp.concatenate([cross, gram], 2), 0)
+    whole = lax.all_gather(half, "core", axis=0, tiled=True)
+    middle = middle_of(whole[:, block : block + columns], whole[:, :block])
+    power = lax.dot_general(
+        tokens, middle, (((1,), (1,)), ((), ())), preferred_element_type=jnp.float32
     )
-    whole = from_everyone(jnp.sum(exchanged(sent, LINE), 0), LINE)
-    cross = whole[:, :share].reshape(block, columns)
-    gram_one = whole[:, share : share + part].reshape(columns, columns)
-    middle = solved(cross, inverse_factor(gram_one)).astype(jnp.bfloat16)
-    power = jnp.dot(tokens, middle, preferred_element_type=jnp.float32)
     power = jnp.sum(exchanged(power.reshape(plane, rows, columns), PLANE), 0)
     powers = from_everyone(power, PLANE).reshape(plane * rows, columns)
     high, low = in_two(powers)
     gram = gram_of(high, low, total)
     cross_two = over_tokens(tokens, high)
-    own = lax.axis_index("core")
     both = lax.all_gather(jnp.concatenate([cross_two, gram]), "core")
     both = both[0] + both[1]
     lines = both[:block].reshape(line // pair, pair, share, columns)
@@ -145,13 +183,9 @@
     lines = lax.dynamic_index_in_dim(lines, own, 1, False)
     half = lax.dynamic_index_in_dim(half, own, 0, False)
     half = jnp.broadcast_to(half, (line // pair, *half.shape))
-    own = jnp.sum(exchanged(jnp.concatenate([lines, half], 1), "z"), 0)
-    cross_two = own[:share]
-    gram_two = lax.all_gather(own[share:], "core", axis=0, tiled=True)
-    inverse_two = inverse_factor(gram_two)
-    basis = solved(power, inverse_two)
-    projected = solved(cross_two, inverse_two) / jnp.sqrt(total)
-    return (basis, projected)
+    summed = jnp.sum(exchanged(jnp.concatenate([lines, half], 1), "z"), 0)
+    gram_two = lax.all_gather(summed[share:], "core", axis=0, tiled=True)
+    return tuple(outputs_of(gram_two, power, summed[:share], total))
 
 
 def solution(mesh):

time: 135 us -> 125 us (0.926)
  blocking collectives: 98.4 us -> 83.2 us
  waiting for transfers between devices: 9.9 us -> 18.3 us
  matrix products: 8.29 us -> 3.8 us
  starting transfers between devices: 3.63 us -> 7.57 us
  Pallas kernels: 8.46 us -> 6.78 us
    all_to_all x5 -> x4, blocking collectives: 91.6 us -> 67.6 us  [exchanged(): return lax.all_to_all(array, axes, 0, 0, tiled=True)]
    all_to_all x1, waiting for transfers between devices: 9.9 us -> 18.3 us  [exchanged(): return lax.all_to_all(array, axes, 0, 0, tiled=True)]
    all_gather x1 -> x3, blocking collectives: 2.51 us -> 10.6 us  [the longest x1 5.2 us: on_device(): both = lax.all_gather(both.reshape(pair, columns // pair, -1), 'core')]
    dot_general x4 -> x1, matrix products: 4.79 us -> 0.36 us  [on_device(): lax.dot_general(tokens, middle, (((1,), (1,)), ((), ())), preferred_eleme...]
    all_to_all x1, starting transfers between devices: 3.63 us -> 7.57 us  [exchanged(): return lax.all_to_all(array, axes, 0, 0, tiled=True)]
    pallas_call x2, Pallas kernels: 8.46 us -> 6.78 us  [the longest x1 3.7 us: outputs_of(): pl.pallas_call(functools.partial(outputs_kernel, scale=float(total) ** (-...]
where the time goes in v4:
time: 125 us
  blocking collectives  83.2 us (67%)
  waiting for transfers between devices  18.3 us (15%)
  starting transfers between devices  7.57 us (6%)
  Pallas kernels  6.78 us (5%)
  matrix products  3.8 us (3%)
  local copies, waits for them, and re-layouts  3.49 us (3%)
    all_to_all x4, blocking collectives, exchanged(): return lax.all_to_all(array, axes, 0, 0, tiled=True)  67.6 us
    all_to_all x1, waiting for transfers between devices, exchanged(): return lax.all_to_all(array, axes, 0, 0, tiled=True)  18.3 us
    all_to_all x1, starting transfers between devices, exchanged(): return lax.all_to_all(array, axes, 0, 0, tiled=True)  7.57 us
    all_gather x1, blocking collectives, on_device(): both = lax.all_gather(both.reshape(pair, columns // pair, -1), 'core')  5.2 us
    all_gather x1, blocking collectives, on_device(): both = lax.all_gather(jnp.concatenate([cross_two, gram]), 'core')  4.97 us
    pallas_call x1, Pallas kernels, outputs_of(): pl.pallas_call(functools.partial(outputs_kernel, scale=float(total) ** (-...  3.7 us
    pallas_call x1, Pallas kernels, middle_of(): pl.pallas_call(middle_kernel, out_shape=pltpu.VMEM(cross.shape, jnp.bfloa...  3.08 us
    all_gather x1, blocking collectives, on_device(): whole = lax.all_gather(half, 'core', axis=0, tiled=True)  3.04 us
  transfers between devices with their start and end apart: 1, of which 1 were waited for; matrix products, arithmetic and copies ran while one was open for 0% of the time, Pallas kernels for 0%

profile of v4, /device:TPU:1, one launch (start us, length us, event | category | flops | bytes accessed | tf_op | source)
XLA Modules:
  0.0 124.6 jit_solution(6181251998403210912)
XLA Ops:
  0.6 0.0 copy-start
  0.6 0.0 copy-start.1
  0.7 1.3 %copy-done = bf16[96,6144]{1,0:T(8,128)(2,1)S(1)} copy-done((bf16[96,6144]{1,0:T(8,128)(2,1)S(1)}, bf16[96,6144]{1,0:T(8,128)(2,1)}, u32[]{:S(2)}) %copy-start) | copy-done | bytes 1179672
  1.9 1.7 %reduce-precision_convert_fusion.1 = (bf16[64,96]{1,0:T(8,128)(2,1)S(1)}, bf16[64,96]{1,0:T(8,128)(2,1)S(1)}) fusion(bf16[64,6144]{1,0:T(8,128)(2,1)} %param.2, bf16[96,6144]{1,0:T(8,128)(2,1)S(1)} %copy-done), kind=kOutput, calls=%fused_computation.39 | convolution fusion | flops 75522048 | bytes 1990656 | tf_op jit(solution)/shard_map/dot_general | solution.py:146
  3.6 0.0 copy-done.1
  3.6 0.1 copy.63
  3.7 0.1 fusion.20
  3.8 0.1 pad_maximum_fusion
  4.0 1.4 %copy.43 = bf16[16,64,640]{2,1,0:T(8,128)(2,1)} copy(bf16[16,64,640]{2,0,1:T(8,128)(2,1)S(1)} %pad_maximum_fusion) | data formatting | bytes 2621440 | tf_op jit(solution)/shard_map/concatenate | solution.py:154
  5.3 7.6 %all-to-all-start = ((bf16[16,64,640]{2,1,0:T(8,128)(2,1)}), bf16[16,64,640]{2,1,0:T(8,128)(2,1)S(1)}, u32[]{:S(2)}, u32[]{:S(2)}) async-start(bf16[16,64,640]{2,1,0:T(8,128)(2,1)} %copy.43), calls=%async_computation | async-start | bytes 2621440 | tf_op jit(solution)/shard_map/all_to_all | solution.py:19
  12.9 18.3 %all-to-all-done = bf16[16,64,640]{2,1,0:T(8,128)(2,1)S(1)} async-done(((bf16[16,64,640]{2,1,0:T(8,128)(2,1)}), bf16[16,64,640]{2,1,0:T(8,128)(2,1)S(1)}, u32[]{:S(2)}, u32[]{:S(2)}) %all-to-all-start) | async-done | bytes 1310752 | tf_op jit(solution)/shard_map/all_to_all | solution.py:19
  31.2 0.3 fusion.11
  31.4 0.3 fusion.5
  31.8 0.3 convolution_add_fusion
  32.1 0.1 copy.46
  32.3 5.2 %all_gather.15 = f32[2,2,48,512]{3,2,1,0:T(8,128)S(1)} all-gather(f32[1,2,48,512]{3,2,1,0:T(8,128)S(1)} %bitcast.48), channel_id=1, replica_groups=mesh['x'=4,'y'=4,'z'=8,'core'=2] {'core'}, dimensions={0}, use_global_device_ids=true | all-gather | bytes 589824 | tf_op jit(solution)/shard_map/all_gather | solution.py:162
  37.6 26.4 %all_to_all.25 = bf16[8,48,768]{2,1,0:T(8,128)(2,1)S(1)} all-to-all(bf16[8,48,768]{2,1,0:T(8,128)(2,1)S(1)} %broadcast_in_dim.13), channel_id=1, replica_groups=mesh['x'=4,'y'=4,'z'=8,'core'=2] {'z'}, dimensions={0} | all-to-all | bytes 1179648 | tf_op jit(solution)/shard_map/all_to_all | solution.py:19
  64.1 3.0 %all_gather.16 = f32[96,512]{1,0:T(8,128)S(1)} all-gather(f32[48,512]{1,0:T(8,128)S(1)} %maximum_reduce_fusion), channel_id=1, replica_groups=mesh['x'=4,'y'=4,'z'=8,'core'=2] {'core'}, dimensions={0}, use_global_device_ids=true | all-gather | bytes 294912 | tf_op jit(solution)/shard_map/all_gather | solution.py:169
  67.2 3.1 %shard_map.41 = bf16[96,384]{1,0:T(8,128)(2,1)S(1)} custom-call(f32[96,96]{1,0:T(8,128)S(1)} %slice.83.gram, f32[96,384]{1,0:T(8,128)S(1)} %slice.84.cross), custom_call_target="tpu_custom_call" | custom-call | tf_op jit(solution)/shard_map/pallas_call | solution.py:98
  70.3 0.4 fusion.3
  70.7 13.4 %all_to_all.26 = f32[16,64,96]{2,1,0:T(8,128)S(1)} all-to-all(f32[16,64,96]{2,1,0:T(8,128)S(1)} %bitcast.47), channel_id=1, replica_groups=mesh['x'=4,'y'=4,'z'=8,'core'=2] {'x','y'}, dimensions={0} | all-to-all | bytes 786432 | tf_op jit(solution)/shard_map/all_to_all | solution.py:19
  84.2 12.7 %all_to_all.27 = f32[16,64,96]{2,1,0:T(8,128)S(1)} all-to-all(f32[16,64,96]{2,1,0:T(8,128)S(1)} %broadcast_in_dim.14), channel_id=1, replica_groups=mesh['x'=4,'y'=4,'z'=8,'core'=2] {'x','y'}, dimensions={0} | all-to-all | bytes 786432 | tf_op jit(solution)/shard_map/all_to_all | solution.py:19
  97.0 0.3 convolution_bitcast_fusion.1
  97.2 0.3 fusion.1
  97.6 0.3 fusion
  97.8 0.1 copy.50
  97.9 0.1 copy.51
  98.0 5.0 %all-gather.1 = f32[2,480,96]{1,2,0:T(8,128)S(1)} all-gather(f32[1,480,96]{1,2,0:T(8,128)S(1)} %maximum_bitcast_fusion), channel_id=2, replica_groups=mesh['x'=4,'y'=4,'z'=8,'core'=2] {'core'}, dimensions={0}, use_global_device_ids=true | all-gather | bytes 552960 | tf_op jit(solution)/shard_map/all_gather | solution.py:179
  103.1 0.1 copy.62
  103.2 0.1 copy.61
  103.5 15.0 %all_to_all.28 = f32[8,72,96]{2,1,0:T(8,128)S(1)} all-to-all(f32[8,72,96]{2,1,0:T(8,128)S(1)} %pad_maximum_fusion.1), channel_id=1, replica_groups=mesh['x'=4,'y'=4,'z'=8,'core'=2] {'z'}, dimensions={0} | all-to-all | bytes 442368 | tf_op jit(solution)/shard_map/all_to_all | solution.py:19
  118.6 2.4 %all_gather.19.gram = f32[96,96]{1,0:T(8,128)S(1)} all-gather(f32[48,96]{1,0:T(8,128)S(1)} %slice.89), channel_id=1, replica_groups=mesh['x'=4,'y'=4,'z'=8,'core'=2] {'core'}, dimensions={0}, use_global_device_ids=true | all-gather | bytes 55296 | tf_op jit(solution)/shard_map/all_gather | solution.py:187
  120.9 3.7 %shard_map.42 = (f32[64,96]{1,0:T(8,128)}, f32[24,96]{1,0:T(8,128)}) custom-call(f32[96,96]{1,0:T(8,128)S(1)} %all_gather.19.gram, f32[64,96]{1,0:T(8,128)S(1)} %reduce_sum.28.power, f32[24,96]{1,0:T(8,128)S(1)} %slice.90.cross_two), custom_call_target="tpu_custom_call" | custom-call | tf_op jit(solution)/shard_map/pallas_call | solution.py:106
  (30 shorter events, 0.7 us)
Async XLA Ops:
  0.6 1.3 %copy-start = (bf16[96,6144]{1,0:T(8,128)(2,1)S(1)}, bf16[96,6144]{1,0:T(8,128)(2,1)}, u32[]{:S(2)}) copy-start(bf16[96,6144]{1,0:T(8,128)(2,1)} %param.3) | copy-start | bytes 3538948
  0.6 2.9 %copy-start.1 = (bf16[64,6144]{1,0:T(8,128)(2,1)S(1)}, bf16[64,6144]{1,0:T(8,128)(2,1)}, u32[]{:S(2)}) copy-start(bf16[64,6144]{1,0:T(8,128)(2,1)} %param.2) | copy-start | bytes 2359300
  5.3 25.8 %all-to-all-start = ((bf16[16,64,640]{2,1,0:T(8,128)(2,1)}), bf16[16,64,640]{2,1,0:T(8,128)(2,1)S(1)}, u32[]{:S(2)}, u32[]{:S(2)}) async-start(bf16[16,64,640]{2,1,0:T(8,128)(2,1)} %copy.43), calls=%async_computation | async-start | bytes 2621440 | tf_op jit(solution)/shard_map/all_to_all | solution.py:19

commit v5 on v4

v5 whole, which is shorter than its diff:
```python
import functools

import jax
import jax.numpy as jnp
from jax import lax
from jax.experimental import pallas as pl
from jax.experimental.pallas import tpu as pltpu
from jax.sharding import Mesh
from jax.sharding import PartitionSpec as P

PLANE = ("x", "y")
LINE = ("z", "core")
EVERY = ("x", "y", "z", "core")
GROUP = 8
LANES = 128
PIECES = 4


def exchanged(array, axes):
    return lax.all_to_all(array, axes, 0, 0, tiled=True)


def from_everyone(array, axes):
    return exchanged(jnp.broadcast_to(array, (lax.axis_size(axes), *array.shape)), axes)


def invert_factor(gram, inverse):
    size = inverse.shape[0]
    shape = (GROUP, size)
    lane = lax.broadcasted_iota(jnp.int32, shape, 1)
    row = lax.broadcasted_iota(jnp.int32, shape, 0)

    def column(value, at):
        return jnp.broadcast_to(value[:, at : at + 1], shape)

    def line(value, at):
        return jnp.broadcast_to(value[at : at + 1], shape)

    groups = [gram[first : first + GROUP, :size] for first in range(0, size, GROUP)]
    for at, own in enumerate(groups):
        first = at * GROUP
        columns = [column(own, first + k) for k in range(GROUP)]
        pivots = jnp.ones(shape, jnp.float32)
        lines, scales, uppers = [], [], {}
        for k in range(GROUP):
            pivot = line(columns[k], k)
            scale = 1.0 / pivot
            pivots = jnp.where(row == k, pivot, pivots)
            factor = jnp.where(row > k, columns[k] * scale, 0.0)
            own = jnp.where((lane == first + k) & (row >= k), jnp.where(row == k, 1.0, 0.0), own)
            lines.append(line(own, k))
            scales.append(scale)
            own = own - factor * lines[k]
            lines[k] = jnp.where((lane > first + k) & (lane < first + GROUP), 0.0, lines[k])
            for j in range(k + 1, GROUP):
                uppers[k, j] = line(columns[j], k)
                columns[j] = columns[j] - factor * uppers[k, j]
        inverse[pl.ds(first, GROUP), :] = jnp.where(
            lane <= first + row, own * lax.rsqrt(pivots), 0.0
        )
        inside = (lane >= first) & (lane < first + GROUP)
        for later in range(at + 1, len(groups)):
            value = groups[later]
            columns = [column(value, first + k) for k in range(GROUP)]
            value = jnp.where(inside, 0.0, value)
            for k in range(GROUP):
                factor = columns[k] * scales[k]
                value = value - factor * lines[k]
                for j in range(k + 1, GROUP):
                    columns[j] = columns[j] - factor * uppers[k, j]
            groups[later] = value

def times(left, right, right_dim):
    return lax.dot_general(
        left,
        right,
        (((1,), (right_dim,)), ((), ())),
        precision=lax.Precision.HIGHEST,
        preferred_element_type=jnp.float32,
    )


def middle_kernel(summed, middle, inverse):
    block = middle.shape[1]
    invert_factor(summed[:, block:], inverse)
    middle[...] = times(inverse[...], summed[:, :block], 0).astype(jnp.bfloat16)


def outputs_kernel(parts, power, basis, projected, inverse, *, scale):
    columns = power.shape[1]
    summed = parts[0]
    for at in range(1, parts.shape[0]):
        summed = summed + parts[at]
    invert_factor(summed, inverse)
    basis[...] = times(power[...], inverse[...], 1)
    own = summed[:, columns : columns + projected.shape[0]]
    projected[...] = times(inverse[...], own, 0).T * scale


def near(*arrays):
    return [pltpu.with_memory_space_constraint(a, pltpu.VMEM) for a in arrays]


def packed_kernel(_, tokens, test_matrix, sent, left, right, signals):
    count, rows, wide = sent.shape
    block = tokens.shape[1] // count
    pieces = signals.shape[1]
    each = count // pieces
    piece = each * block
    spans = [pl.ds(at * piece, piece) for at in range(pieces)]
    copies = [
        [
            pltpu.make_async_copy(source.at[:, spans[at]], held.at[:, spans[at]], signal.at[at])
            for at in range(pieces)
        ]
        for source, held, signal in (
            (tokens, left, signals.at[0]),
            (test_matrix, right, signals.at[1]),
        )
    ]
    for pair in zip(*copies, strict=True):
        for copy in pair:
            copy.start()
    sketch = jnp.zeros((rows, test_matrix.shape[0]), jnp.float32)
    for at, pair in enumerate(zip(*copies, strict=True)):
        for copy in pair:
            copy.wait()
        sketch += lax.dot_general(
            left[:, spans[at]],
            right[:, spans[at]],
            (((1,), (1,)), ((), ())),
            preferred_element_type=jnp.float32,
        )
        for to in range(at * each, (at + 1) * each):
            sent[to, :, :block] = left[:, to * block : (to + 1) * block]
    high = sketch.astype(jnp.bfloat16)
    low = (sketch - high.astype(jnp.float32)).astype(jnp.bfloat16)
    spare = jnp.zeros((rows, wide - block - 2 * sketch.shape[1]), jnp.bfloat16)
    tail = jnp.concatenate([high, low, spare], 1)
    for to in range(count):
        sent[to, :, block:] = tail


def packed(own, tokens, test_matrix, count):
    rows, width = tokens.shape
    wide = width // count + 2 * test_matrix.shape[0]
    return pl.pallas_call(
        packed_kernel,
        in_specs=[
            pl.BlockSpec(memory_space=pltpu.SMEM),
            pl.BlockSpec(memory_space=pl.ANY),
            pl.BlockSpec(memory_space=pl.ANY),
        ],
        out_shape=pltpu.VMEM((count, rows, wide + -wide % LANES), jnp.bfloat16),
        scratch_shapes=[
            pltpu.VMEM(tokens.shape, tokens.dtype),
            pltpu.VMEM(test_matrix.shape, test_matrix.dtype),
            pltpu.SemaphoreType.DMA((2, PIECES)),
        ],
    )(own, tokens, test_matrix)


def over_rows(left, right):
    return lax.dot_general(
        left, right, (((0,), (0,)), ((), ())), preferred_element_type=jnp.float32
    )


def cross_kernel(mixed, both, *, block, scale):
    columns = both.shape[0]
    high = mixed[:, block : block + columns]
    product = over_rows(high, mixed[...])
    gram = product[:, block : block + columns] + product[:, block + columns : block + 2 * columns]
    spare = jnp.zeros((columns, both.shape[1] - block - columns), jnp.float32)
    both[:, :block] = product[:, :block]
    both[:, block:] = jnp.concatenate([(gram + gram.T) * scale, spare], 1)


def cross_of(mixed, columns, block, total):
    return pl.pallas_call(
        functools.partial(cross_kernel, block=block, scale=0.5 / total),
        out_shape=pltpu.VMEM((columns, block + columns + -columns % LANES), jnp.float32),
    )(*near(mixed))


def cross_two_kernel(mixed, powers, both, *, block, scale):
    columns = both.shape[0]
    exact = powers[...]
    high = exact.astype(jnp.bfloat16)
    low = (exact - high.astype(jnp.float32)).astype(jnp.bfloat16)
    gram = over_rows(high, high) + over_rows(high, low)
    spare = jnp.zeros((columns, both.shape[1] - block - columns), jnp.float32)
    both[:, :block] = over_rows(high, mixed[:, :block])
    both[:, block:] = jnp.concatenate([(gram + gram.T) * scale, spare], 1)


def cross_two_of(mixed, powers, block, total):
    columns = powers.shape[1]
    return pl.pallas_call(
        functools.partial(cross_two_kernel, block=block, scale=0.5 / total),
        out_shape=pltpu.VMEM((columns, block + columns + -columns % LANES), jnp.float32),
    )(*near(mixed, powers))


def middle_of(summed, block):
    columns = summed.shape[0]
    return pl.pallas_call(
        middle_kernel,
        out_shape=pltpu.VMEM((columns, block), jnp.bfloat16),
        scratch_shapes=[pltpu.VMEM((columns, columns), jnp.float32)],
    )(*near(summed))


def outputs_of(parts, power, share, total):
    columns = power.shape[1]
    return pl.pallas_call(
        functools.partial(outputs_kernel, scale=total**-0.5),
        out_shape=[
            jax.ShapeDtypeStruct(power.shape, jnp.float32),
            jax.ShapeDtypeStruct((share, columns), jnp.float32),
        ],
        scratch_shapes=[pltpu.VMEM((columns, columns), jnp.float32)],
    )(*near(parts, power))


def spread_kernel(own, both, sent, *, block, share):
    columns = both.shape[1]
    summed = both[0] + both[1]
    gram = summed[:, block : block + columns]
    lines = summed[:, :block]
    lines = jnp.where(own[0] == 0, lines, pltpu.roll(lines, block - share, 1))
    spare = jnp.zeros((columns, sent.shape[2] - columns - share), jnp.float32)
    for to in range(sent.shape[0]):
        first = 2 * share * to
        sent[to] = jnp.concatenate([gram, lines[:, first : first + share], spare], 1)


def spread(both, own, line, share):
    columns = both.shape[1]
    lanes = columns + share
    return pl.pallas_call(
        functools.partial(spread_kernel, block=line * share, share=share),
        in_specs=[pl.BlockSpec(memory_space=pltpu.SMEM), pl.BlockSpec()],
        out_shape=pltpu.VMEM((line // 2, columns, lanes + -lanes % LANES), jnp.float32),
    )(own, *near(both))


def in_three(array):
    high = lax.reduce_precision(array, 8, 7)
    rest = array - high
    middle = lax.reduce_precision(rest, 8, 7)
    return [part.astype(jnp.bfloat16) for part in (high, middle, rest - middle)]


def on_device(tokens_x, test_matrix):
    rows, width = tokens_x.shape
    columns = test_matrix.shape[0]
    plane, line, pair = (lax.axis_size(a) for a in (PLANE, LINE, "core"))
    total = rows * plane * line
    block = width // plane
    share = block // line
    own = lax.axis_index("core").reshape(1)
    sent = packed(own, tokens_x, test_matrix, plane)
    mixed = exchanged(sent, PLANE).reshape(plane * rows, -1)
    both = cross_of(mixed, columns, block, total)
    both = lax.all_gather(both.reshape(pair, columns // pair, -1), "core")
    half = lax.dynamic_index_in_dim(both[0] + both[1], own[0], 0, False)
    cross = half[:, :block].astype(jnp.bfloat16)
    sent = from_everyone(jnp.concatenate([cross, *in_three(half[:, block:])], 1), "z")
    cross = sent[:, :, :block].astype(jnp.float32)
    gram = sum(part.astype(jnp.float32) for part in jnp.split(sent[:, :, block:], 3, 2))
    half = jnp.sum(jnp.concatenate([cross, gram], 2), 0)
    whole = lax.all_gather(half, "core", axis=0, tiled=True)
    middle = middle_of(whole, block)
    power = lax.dot_general(
        mixed[:, :block],
        middle,
        (((1,), (1,)), ((), ())),
        preferred_element_type=jnp.float32,
    )
    power = jnp.sum(exchanged(power.reshape(plane, rows, columns), PLANE), 0)
    powers = from_everyone(power, PLANE).reshape(plane * rows, columns)
    both = lax.all_gather(cross_two_of(mixed, powers, block, total), "core")
    parts = exchanged(spread(both, own, line, share), "z")
    return tuple(outputs_of(parts, power, share, total))


def solution(mesh):
    finer = Mesh(mesh.devices.reshape(4, 4, 8, mesh.shape["sub"]), EVERY)
    return jax.shard_map(
        on_device,
        mesh=finer,
        in_specs=(P(EVERY, None), P()),
        out_specs=(P(EVERY, None), P(EVERY, None)),
        check_vma=False,
    )
```

time: 125 us -> 122 us (0.976)
  Pallas kernels: 6.78 us -> 11.4 us
  matrix products: 3.8 us -> 0.36 us
  local copies, waits for them, and re-layouts: 3.49 us -> 0.12 us
    pallas_call x2 -> x6, Pallas kernels: 6.78 us -> 11.4 us  [the longest x1 3.72 us: outputs_of(): pl.pallas_call(functools.partial(outputs_kernel, scale=total ** (-0.5)),...]
    dot_general x8 -> x1, matrix products: 3.8 us -> 0.36 us  [on_device(): lax.dot_general(mixed[:, :block], middle, (((1,), (1,)), ((), ())), prefe...]
    all_to_all x4, blocking collectives: 67.6 us -> 70.1 us  [exchanged(): return lax.all_to_all(array, axes, 0, 0, tiled=True)]
    all_gather x2 -> x1, blocking collectives: 7.35 us -> 4.98 us  [on_device(): both = lax.all_gather(cross_two_of(mixed, powers, block, total), 'core')]
    unnamed x7 -> x0, local copies, waits for them, and re-layouts: 1.62 us -> none
    concatenate x1 -> x0, local copies, waits for them, and re-layouts: 1.35 us -> none  [on_device(): jnp.concatenate([blocks, own], 2)]
where the time goes in v5:
time: 122 us
  blocking collectives  83.3 us (68%)
  waiting for transfers between devices  18.3 us (15%)
  Pallas kernels  11.4 us (9%)
  starting transfers between devices  7.58 us (6%)
    all_to_all x4, blocking collectives, exchanged(): return lax.all_to_all(array, axes, 0, 0, tiled=True)  70.1 us
    all_to_all x1, waiting for transfers between devices, exchanged(): return lax.all_to_all(array, axes, 0, 0, tiled=True)  18.3 us
    all_to_all x1, starting transfers between devices, exchanged(): return lax.all_to_all(array, axes, 0, 0, tiled=True)  7.58 us
    all_gather x1, blocking collectives, on_device(): both = lax.all_gather(both.reshape(pair, columns // pair, -1), 'core')  5.21 us
    all_gather x1, blocking collectives, on_device(): both = lax.all_gather(cross_two_of(mixed, powers, block, total), 'core')  4.98 us
    pallas_call x1, Pallas kernels, outputs_of(): pl.pallas_call(functools.partial(outputs_kernel, scale=total ** (-0.5)),...  3.72 us
    pallas_call x1, Pallas kernels, packed(): pl.pallas_call(packed_kernel, in_specs=[pl.BlockSpec(memory_space=pltpu.S...  3.4 us
    pallas_call x1, Pallas kernels, middle_of(): pl.pallas_call(middle_kernel, out_shape=pltpu.VMEM((columns, block), jnp....  3.08 us
  transfers between devices with their start and end apart: 1, of which 1 were waited for; matrix products, arithmetic and copies ran while one was open for 0% of the time, Pallas kernels for 0%

profile of v5, /device:TPU:1, one launch (start us, length us, event | category | flops | bytes accessed | tf_op | source)
XLA Modules:
  0.0 122.0 jit_solution(1772616794404125057)
XLA Ops:
  0.6 3.4 %shard_map.41 = bf16[16,64,640]{2,1,0:T(8,128)(2,1)} custom-call(s32[1]{0:T(128)} %bitcast._.own, bf16[64,6144]{1,0:T(8,128)(2,1)} %tokens.1, bf16[96,6144]{1,0:T(8,128)(2,1)} %test_matrix.1), custom_call_target="tpu_custom_call" | custom-call | tf_op jit(solution)/shard_map/pallas_call | solution.py:147
  4.0 7.6 %all-to-all-start = ((bf16[16,64,640]{2,1,0:T(8,128)(2,1)}), bf16[16,64,640]{2,1,0:T(8,128)(2,1)S(1)}, u32[]{:S(2)}, u32[]{:S(2)}) async-start(bf16[16,64,640]{2,1,0:T(8,128)(2,1)} %shard_map.41), calls=%async_computation | async-start | bytes 2621440 | tf_op jit(solution)/shard_map/all_to_all | solution.py:20
  11.6 18.3 %all-to-all-done = bf16[16,64,640]{2,1,0:T(8,128)(2,1)S(1)} async-done(((bf16[16,64,640]{2,1,0:T(8,128)(2,1)}), bf16[16,64,640]{2,1,0:T(8,128)(2,1)S(1)}, u32[]{:S(2)}, u32[]{:S(2)}) %all-to-all-start) | async-done | bytes 1310752 | tf_op jit(solution)/shard_map/all_to_all | solution.py:20
  29.9 0.5 shard_map.42
  30.4 5.2 %all_gather.12 = f32[2,2,48,512]{3,2,1,0:T(8,128)S(1)} all-gather(f32[1,2,48,512]{3,2,1,0:T(8,128)S(1)} %bitcast.14), channel_id=1, replica_groups=mesh['x'=4,'y'=4,'z'=8,'core'=2] {'core'}, dimensions={0}, use_global_device_ids=true | all-gather | bytes 589824 | tf_op jit(solution)/shard_map/all_gather | solution.py:266
  35.8 26.4 %all_to_all.25 = bf16[8,48,768]{2,1,0:T(8,128)(2,1)S(1)} all-to-all(bf16[8,48,768]{2,1,0:T(8,128)(2,1)S(1)} %broadcast_in_dim.6), channel_id=1, replica_groups=mesh['x'=4,'y'=4,'z'=8,'core'=2] {'z'}, dimensions={0} | all-to-all | bytes 1179648 | tf_op jit(solution)/shard_map/all_to_all | solution.py:20
  62.3 3.0 %all_gather.13.summed = f32[96,512]{1,0:T(8,128)S(1)} all-gather(f32[48,512]{1,0:T(8,128)S(1)} %maximum_reduce_fusion), channel_id=1, replica_groups=mesh['x'=4,'y'=4,'z'=8,'core'=2] {'core'}, dimensions={0}, use_global_device_ids=true | all-gather | bytes 294912 | tf_op jit(solution)/shard_map/all_gather | solution.py:273
  65.3 3.1 %shard_map.43 = bf16[96,384]{1,0:T(8,128)(2,1)S(1)} custom-call(f32[96,512]{1,0:T(8,128)S(1)} %all_gather.13.summed), custom_call_target="tpu_custom_call" | custom-call | tf_op jit(solution)/shard_map/pallas_call | solution.py:207
  68.4 0.4 fusion
  68.8 13.4 %all_to_all.26 = f32[16,64,96]{2,1,0:T(8,128)S(1)} all-to-all(f32[16,64,96]{2,1,0:T(8,128)S(1)} %bitcast.15), channel_id=1, replica_groups=mesh['x'=4,'y'=4,'z'=8,'core'=2] {'x','y'}, dimensions={0} | all-to-all | bytes 786432 | tf_op jit(solution)/shard_map/all_to_all | solution.py:20
  82.3 12.7 %all_to_all.27 = f32[16,64,96]{2,1,0:T(8,128)S(1)} all-to-all(f32[16,64,96]{2,1,0:T(8,128)S(1)} %broadcast_in_dim.7), channel_id=1, replica_groups=mesh['x'=4,'y'=4,'z'=8,'core'=2] {'x','y'}, dimensions={0} | all-to-all | bytes 786432 | tf_op jit(solution)/shard_map/all_to_all | solution.py:20
  95.1 0.4 shard_map.44
  95.5 5.0 %all-gather = f32[192,512]{1,0:T(8,128)S(1)} all-gather(f32[96,512]{1,0:T(8,128)S(1)} %shard_map.44), channel_id=2, replica_groups=mesh['x'=4,'y'=4,'z'=8,'core'=2] {'core'}, dimensions={0}, use_global_device_ids=true | all-gather | bytes 589824 | tf_op jit(solution)/shard_map/all_gather | solution.py:283
  100.5 0.2 shard_map.45
  100.7 17.5 %all_to_all.28.parts = f32[8,96,128]{2,1,0:T(8,128)S(1)} all-to-all(f32[8,96,128]{2,1,0:T(8,128)S(1)} %shard_map.45), channel_id=1, replica_groups=mesh['x'=4,'y'=4,'z'=8,'core'=2] {'z'}, dimensions={0} | all-to-all | bytes 786432 | tf_op jit(solution)/shard_map/all_to_all | solution.py:20
  118.2 3.7 %shard_map.46 = (f32[64,96]{1,0:T(8,128)}, f32[24,96]{1,0:T(8,128)}) custom-call(f32[8,96,128]{2,1,0:T(8,128)S(1)} %all_to_all.28.parts, f32[64,96]{1,0:T(8,128)S(1)} %reduce_sum.19.power), custom_call_target="tpu_custom_call" | custom-call | tf_op jit(solution)/shard_map/pallas_call | solution.py:216
  (11 shorter events, 0.3 us)
Async XLA Ops:
  4.0 25.9 %all-to-all-start = ((bf16[16,64,640]{2,1,0:T(8,128)(2,1)}), bf16[16,64,640]{2,1,0:T(8,128)(2,1)S(1)}, u32[]{:S(2)}, u32[]{:S(2)}) async-start(bf16[16,64,640]{2,1,0:T(8,128)(2,1)} %shard_map.41), calls=%async_computation | async-start | bytes 2621440 | tf_op jit(solution)/shard_map/all_to_all | solution.py:20

commit v6 on v5

v6 whole, which is shorter than its diff:
```python
import functools

import jax
import jax.numpy as jnp
from jax import lax
from jax.experimental import pallas as pl
from jax.experimental.pallas import tpu as pltpu
from jax.sharding import Mesh
from jax.sharding import PartitionSpec as P

PLANE = ("x", "y")
LINE = ("z", "core")
EVERY = ("x", "y", "z", "core")
GROUP = 8
LANES = 128
PIECES = 4


def exchanged(array, axes):
    return lax.all_to_all(array, axes, 0, 0, tiled=True)


def traded(array):
    return lax.ppermute(array, "core", [(0, 1), (1, 0)])


def in_two(array):
    high = array.astype(jnp.bfloat16)
    return high, (array - high.astype(jnp.float32)).astype(jnp.bfloat16)


def in_three(array):
    high = array.astype(jnp.bfloat16)
    rest = array - high.astype(jnp.float32)
    middle, low = in_two(rest)
    return high, middle, low


def invert_factor(gram, inverse):
    size = inverse.shape[0]
    shape = (GROUP, size)
    lane = lax.broadcasted_iota(jnp.int32, shape, 1)
    row = lax.broadcasted_iota(jnp.int32, shape, 0)

    def column(value, at):
        return jnp.broadcast_to(value[:, at : at + 1], shape)

    def line(value, at):
        return jnp.broadcast_to(value[at : at + 1], shape)

    groups = [gram[first : first + GROUP, :size] for first in range(0, size, GROUP)]
    for at, own in enumerate(groups):
        first = at * GROUP
        columns = [column(own, first + k) for k in range(GROUP)]
        pivots = jnp.ones(shape, jnp.float32)
        lines, scales, uppers = [], [], {}
        for k in range(GROUP):
            pivot = line(columns[k], k)
            scale = 1.0 / pivot
            pivots = jnp.where(row == k, pivot, pivots)
            factor = jnp.where(row > k, columns[k] * scale, 0.0)
            own = jnp.where((lane == first + k) & (row >= k), jnp.where(row == k, 1.0, 0.0), own)
            lines.append(line(own, k))
            scales.append(scale)
            own = own - factor * lines[k]
            lines[k] = jnp.where((lane > first + k) & (lane < first + GROUP), 0.0, lines[k])
            for j in range(k + 1, GROUP):
                uppers[k, j] = line(columns[j], k)
                columns[j] = columns[j] - factor * uppers[k, j]
        inverse[pl.ds(first, GROUP), :] = jnp.where(
            lane <= first + row, own * lax.rsqrt(pivots), 0.0
        )
        inside = (lane >= first) & (lane < first + GROUP)
        for later in range(at + 1, len(groups)):
            value = groups[later]
            columns = [column(value, first + k) for k in range(GROUP)]
            value = jnp.where(inside, 0.0, value)
            for k in range(GROUP):
                factor = columns[k] * scales[k]
                value = value - factor * lines[k]
                for j in range(k + 1, GROUP):
                    columns[j] = columns[j] - factor * uppers[k, j]
            groups[later] = value

def times(left, right, right_dim):
    return lax.dot_general(
        left,
        right,
        (((1,), (right_dim,)), ((), ())),
        precision=lax.Precision.HIGHEST,
        preferred_element_type=jnp.float32,
    )


def over_rows(left, right):
    return lax.dot_general(
        left, right, (((0,), (0,)), ((), ())), preferred_element_type=jnp.float32
    )


def corners(size):
    shape = (size, size)
    return lax.broadcasted_iota(jnp.int32, shape, 0), lax.broadcasted_iota(jnp.int32, shape, 1)


def halves_of(gram):
    size = gram.shape[0] // 2
    row, column = corners(size)
    last = gram[size:, size:]
    mixed = jnp.where(row >= column, gram[:size, :size], last)
    diagonal = jnp.sum(jnp.where(row == column, last, 0.0), 1, keepdims=True)
    return gram[size:, :size], mixed, diagonal


def gram_from(square, mixed, diagonal):
    row, column = corners(square.shape[0])
    under = jnp.where(row > column, mixed, 0.0)
    over = jnp.where(row < column, mixed, 0.0)
    first = under + under.T + jnp.where(row == column, mixed, 0.0)
    last = over + over.T + jnp.where(row == column, diagonal, 0.0)
    top = jnp.concatenate([first, square.T], 1)
    return jnp.concatenate([top, jnp.concatenate([square, last], 1)], 0)


def widened(array, lanes=LANES):
    rows, width = array.shape
    return jnp.concatenate([array, jnp.zeros((rows, lanes - width), array.dtype)], 1)


def folded(square, diagonal):
    both = jnp.concatenate([square, diagonal], 1)
    rows = both.shape[0] // 2
    return widened(jnp.concatenate([both[:rows], both[rows:]], 1))


def unfolded(array, size):
    both = jnp.concatenate([array[:, : size + 1], array[:, size + 1 : 2 * size + 2]], 0)
    return both[:, :size], both[:, size:]


def dense(array):
    width = array.shape[1]
    spare = LANES - width
    rows = array.shape[0] * width // LANES
    rest = array[rows:]
    side = jnp.concatenate([rest[:, at : at + spare] for at in range(0, width, spare)], 0)
    return jnp.concatenate([array[:rows], side], 1)


def undense(array, width):
    spare = LANES - width
    side = array[:, width:]
    each = array.shape[0] * spare // width
    parts = [side[at : at + each] for at in range(0, side.shape[0], each)]
    return jnp.concatenate([array[:, :width], jnp.concatenate(parts, 1)], 0)


def near(*arrays):
    return [pltpu.with_memory_space_constraint(a, pltpu.VMEM) for a in arrays]


def whole(count):
    return [pl.BlockSpec(memory_space=pltpu.SMEM)] + [pl.BlockSpec()] * count


def packed_kernel(_, tokens, test_matrix, sent, left, right, signals):
    count, _, block = sent.shape
    rows = tokens.shape[0]
    pieces = signals.shape[1]
    each = count // pieces
    piece = each * block
    spans = [pl.ds(at * piece, piece) for at in range(pieces)]
    copies = [
        [
            pltpu.make_async_copy(source.at[:, spans[at]], held.at[:, spans[at]], signal.at[at])
            for at in range(pieces)
        ]
        for source, held, signal in (
            (tokens, left, signals.at[0]),
            (test_matrix, right, signals.at[1]),
        )
    ]
    for pair in zip(*copies, strict=True):
        for copy in pair:
            copy.start()
    sketch = jnp.zeros((rows, test_matrix.shape[0]), jnp.float32)
    for at, pair in enumerate(zip(*copies, strict=True)):
        for copy in pair:
            copy.wait()
        sketch += lax.dot_general(
            left[:, spans[at]],
            right[:, spans[at]],
            (((1,), (1,)), ((), ())),
            preferred_element_type=jnp.float32,
        )
        for to in range(at * each, (at + 1) * each):
            sent[to, :rows] = left[:, to * block : (to + 1) * block]
    high, low = in_two(sketch)
    half = rows // 2
    side = jnp.concatenate([high[:half], low[:half], high[half:], low[half:]], 1)
    for to in range(count):
        sent[to, rows:] = side


def packed(own, tokens, test_matrix, count):
    rows, width = tokens.shape
    return pl.pallas_call(
        packed_kernel,
        in_specs=[
            pl.BlockSpec(memory_space=pltpu.SMEM),
            pl.BlockSpec(memory_space=pl.ANY),
            pl.BlockSpec(memory_space=pl.ANY),
        ],
        out_shape=pltpu.VMEM((count, rows + rows // 2, width // count), jnp.bfloat16),
        scratch_shapes=[
            pltpu.VMEM(tokens.shape, tokens.dtype),
            pltpu.VMEM(test_matrix.shape, test_matrix.dtype),
            pltpu.SemaphoreType.DMA((2, PIECES)),
        ],
    )(own, tokens, test_matrix)


def chosen(own, zero, one):
    return jnp.where(own[0] == 0, zero, one), jnp.where(own[0] == 0, one, zero)


def cross_kernel(own, mixed, keep, give, *, rows, scale):
    count, tall, block = mixed.shape
    columns = block // 4
    size = columns // 2
    half = rows // 2
    flat = (count * half, block)
    side = mixed[:, rows:].reshape(flat)
    cross = over_rows(side[:, :columns], mixed[:, :half].reshape(flat))
    skip = 2 * columns // LANES * LANES
    start = 2 * columns - skip
    again = over_rows(side[:, skip:], mixed[:, half:rows].reshape(flat))
    cross += again[start : start + columns]
    square = over_rows(side, side)
    gram = jnp.zeros((columns, columns), jnp.float32)
    for first in (0, 2 * columns):
        own_rows = square[first : first + columns]
        gram += own_rows[:, first : first + columns]
        gram += own_rows[:, first + columns : first + 2 * columns]
    lower, both, diagonal = halves_of((gram + gram.T) * scale)
    grams = folded(lower, jnp.zeros_like(diagonal)), folded(both, diagonal)
    keep[:size], give[:size] = chosen(own, cross[:size], cross[size:])
    keep[size:], give[size:] = (widened(a, block) for a in chosen(own, *grams))


def cross_of(own, mixed, rows, total):
    count, _, block = mixed.shape
    size = block // 8
    shape = pltpu.VMEM((size + size // 2, block), jnp.float32)
    return pl.pallas_call(
        functools.partial(cross_kernel, rows=rows, scale=0.5 / total),
        in_specs=whole(1),
        out_shape=[shape, shape],
    )(own, *near(mixed))


def spread_kernel(keep, got, sent, *, size):
    cross = (keep[:size] + got[:size]).astype(jnp.bfloat16)
    gram = keep[size:, :LANES] + got[size:, :LANES]
    parts = jnp.concatenate(in_three(gram), 1)
    for to in range(sent.shape[0]):
        sent[to, :size] = cross
        sent[to, size:] = parts


def spread(keep, got, count, size):
    return pl.pallas_call(
        functools.partial(spread_kernel, size=size),
        out_shape=pltpu.VMEM((count, *keep.shape), jnp.bfloat16),
    )(*near(keep, got))


def summed_kernel(parts, half, *, size):
    total = parts[0].astype(jnp.float32)
    for at in range(1, parts.shape[0]):
        total += parts[at].astype(jnp.float32)
    gram = total[size:]
    half[:size] = total[:size]
    gram = gram[:, :LANES] + gram[:, LANES : 2 * LANES] + gram[:, 2 * LANES :]
    half[size:] = widened(gram, half.shape[1])


def summed(parts, size):
    return pl.pallas_call(
        functools.partial(summed_kernel, size=size),
        out_shape=pltpu.VMEM(parts.shape[1:], jnp.float32),
    )(*near(parts))


def power_kernel(own, mixed, mine, other, sent, inverse, *, rows):
    count, _, block = mixed.shape
    size = inverse.shape[0] // 2
    first, second = chosen(own, mine[...], other[...])
    lower, _ = unfolded(first[size:, :LANES], size)
    both, diagonal = unfolded(second[size:, :LANES], size)
    invert_factor(gram_from(lower, both, diagonal), inverse)
    cross = jnp.concatenate([first[:size], second[:size]], 0)
    middle = times(inverse[...], cross, 0).astype(jnp.bfloat16)
    power = lax.dot_general(
        mixed[:, :rows].reshape(count * rows, block),
        middle,
        (((1,), (1,)), ((), ())),
        preferred_element_type=jnp.float32,
    )
    for to in range(count):
        sent[to] = dense(power[to * rows : (to + 1) * rows])


def power_of(own, mixed, mine, other, rows):
    count, _, block = mixed.shape
    columns = block // 4
    return pl.pallas_call(
        functools.partial(power_kernel, rows=rows),
        in_specs=whole(3),
        out_shape=pltpu.VMEM((count, rows * columns // LANES, LANES), jnp.float32),
        scratch_shapes=[pltpu.VMEM((columns, columns), jnp.float32)],
    )(own, *near(mixed, mine, other))


def cross_two_kernel(own, mixed, powers, keep, give, *, rows, scale):
    count, _, block = mixed.shape
    columns = block // 4
    size = columns // 2
    share = columns // 4
    exact = jnp.concatenate([undense(powers[at], columns) for at in range(count)], 0)
    high, low = in_two(exact)
    gram = over_rows(high, high) + over_rows(high, low)
    lower, both, diagonal = halves_of((gram + gram.T) * scale)
    keep[:size] = widened(jnp.concatenate([lower, both, diagonal], 1))
    give[:size] = keep[:size]
    lines = widened(over_rows(high, mixed[:, :rows].reshape(count * rows, block)).T)
    for at in range(block // (2 * share)):
        first = 2 * share * at
        pair = lines[first : first + share], lines[first + share : first + 2 * share]
        place = pl.ds(size + share * at, share)
        keep[place], give[place] = chosen(own, *pair)


def cross_two_of(own, mixed, powers, rows, total):
    _, _, block = mixed.shape
    shape = pltpu.VMEM((block // 8 + block // 2, LANES), jnp.float32)
    return pl.pallas_call(
        functools.partial(cross_two_kernel, rows=rows, scale=0.5 / total),
        in_specs=whole(2),
        out_shape=[shape, shape],
    )(own, *near(mixed, powers))


def spread_two_kernel(keep, got, sent, *, size):
    share = size // 2
    gram = keep[:size] + got[:size]
    for to in range(sent.shape[0]):
        place = pl.ds(size + share * to, share)
        sent[to, :size] = gram
        sent[to, size:] = keep[place] + got[place]


def spread_two(keep, got, count, size):
    return pl.pallas_call(
        functools.partial(spread_two_kernel, size=size),
        out_shape=pltpu.VMEM((count, size + size // 2, LANES), jnp.float32),
    )(*near(keep, got))


def outputs_kernel(parts, power, basis, projected, inverse, *, scale):
    columns = inverse.shape[0]
    size = columns // 2
    total = parts[0]
    for at in range(1, parts.shape[0]):
        total += parts[at]
    lower, both = total[:size, :size], total[:size, size:columns]
    invert_factor(gram_from(lower, both, total[:size, columns : columns + 1]), inverse)
    basis[...] = times(undense(power[...], columns), inverse[...], 1)
    projected[...] = times(total[size:, :columns], inverse[...], 1) * scale


def outputs_of(parts, power, rows, columns, total):
    return pl.pallas_call(
        functools.partial(outputs_kernel, scale=total**-0.5),
        out_shape=[
            jax.ShapeDtypeStruct((rows, columns), jnp.float32),
            jax.ShapeDtypeStruct((columns // 4, columns), jnp.float32),
        ],
        scratch_shapes=[pltpu.VMEM((columns, columns), jnp.float32)],
    )(*near(parts, power))


def on_device(tokens_x, test_matrix):
    rows = tokens_x.shape[0]
    columns = test_matrix.shape[0]
    size = columns // 2
    plane, line = lax.axis_size(PLANE), lax.axis_size("z")
    total = rows * lax.axis_size(EVERY)
    own = lax.axis_index("core").reshape(1)
    mixed = exchanged(packed(own, tokens_x, test_matrix, plane), PLANE)
    keep, give = cross_of(own, mixed, rows, total)
    half = summed(exchanged(spread(keep, traded(give), line, size), "z"), size)
    power = power_of(own, mixed, half, traded(half), rows)
    power = jnp.sum(exchanged(power, PLANE), 0)
    powers = exchanged(jnp.broadcast_to(power, (plane, *power.shape)), PLANE)
    keep, give = cross_two_of(own, mixed, powers, rows, total)
    parts = exchanged(spread_two(keep, traded(give), line, size), "z")
    return tuple(outputs_of(parts, power, rows, columns, total))


def solution(mesh):
    finer = Mesh(mesh.devices.reshape(4, 4, 8, mesh.shape["sub"]), EVERY)
    return jax.shard_map(
        on_device,
        mesh=finer,
        in_specs=(P(EVERY, None), P()),
        out_specs=(P(EVERY, None), P(EVERY, None)),
        check_vma=False,
    )
```

time: 122 us -> 110 us (0.902)
  waiting for transfers between devices: 18.3 us -> 2.9 us
  blocking collectives: 83.3 us -> 86.4 us
    all_to_all x1 -> x0, waiting for transfers between devices: 18.3 us -> none  [exchanged(): return lax.all_to_all(array, axes, 0, 0, tiled=True)]
    all_to_all x4 -> x5, blocking collectives: 70.1 us -> 86.4 us  [exchanged(): return lax.all_to_all(array, axes, 0, 0, tiled=True)]
    all_gather x3 -> x0, blocking collectives: 13.2 us -> none  [the longest x1 5.21 us: on_device(): both = lax.all_gather(both.reshape(pair, columns // pair, -1), 'core')]
    all_to_all x1 -> x0, starting transfers between devices: 7.58 us -> none  [exchanged(): return lax.all_to_all(array, axes, 0, 0, tiled=True)]
    ppermute x0 -> x3, starting transfers between devices: none -> 6.85 us  [traded(): return lax.ppermute(array, 'core', [(0, 1), (1, 0)])]
    ppermute x0 -> x3, waiting for transfers between devices: none -> 2.9 us  [traded(): return lax.ppermute(array, 'core', [(0, 1), (1, 0)])]
    pallas_call x4 -> x6, Pallas kernels: 4.27 us -> 5.98 us  [the longest x1 3.94 us: power_of(): pl.pallas_call(functools.partial(power_kernel, rows=rows), in_specs=whole...]
  transfers between devices with their start and end apart: 1 -> 3, of which waited for: 1 -> 3; matrix products, arithmetic and copies ran while one was open for 0% -> 0% of each run, Pallas kernels for 0% -> 0%
where the time goes in v6:
time: 110 us; the launch traced here: 109 us
  blocking collectives  86.4 us (79%)
  Pallas kernels  12.3 us (11%)
  starting transfers between devices  6.85 us (6%)
  waiting for transfers between devices  2.9 us (3%)
    all_to_all x5, blocking collectives, exchanged(): return lax.all_to_all(array, axes, 0, 0, tiled=True)  86.4 us
    ppermute x3, starting transfers between devices, traded(): return lax.ppermute(array, 'core', [(0, 1), (1, 0)])  6.85 us
    pallas_call x1, Pallas kernels, outputs_of(): pl.pallas_call(functools.partial(outputs_kernel, scale=total ** (-0.5)),...  4 us
    pallas_call x1, Pallas kernels, power_of(): pl.pallas_call(functools.partial(power_kernel, rows=rows), in_specs=whole...  3.94 us
    ppermute x3, waiting for transfers between devices, traded(): return lax.ppermute(array, 'core', [(0, 1), (1, 0)])  2.9 us
    pallas_call x1, Pallas kernels, packed(): pl.pallas_call(packed_kernel, in_specs=[pl.BlockSpec(memory_space=pltpu.S...  2.36 us
  transfers between devices with their start and end apart: 3, of which 3 were waited for; matrix products, arithmetic and copies ran while one was open for 0% of the time, Pallas kernels for 0%

profile of v6, /device:TPU:1, one launch (start us, length us, event | category | flops | bytes accessed | tf_op | source)
XLA Modules:
  0.0 109.2 jit_solution(4410572563303552350)
XLA Ops:
  0.6 2.4 %shard_map.41 = bf16[16,96,384]{2,1,0:T(8,128)(2,1)S(1)} custom-call(s32[1]{0:T(128)} %bitcast._.own, bf16[64,6144]{1,0:T(8,128)(2,1)} %tokens.1, bf16[96,6144]{1,0:T(8,128)(2,1)} %test_matrix.1), custom_call_target="tpu_custom_call" | custom-call | tf_op jit(solution)/shard_map/pallas_call | solution.py:207
  3.0 24.8 %all_to_all.25.mixed = bf16[16,96,384]{2,1,0:T(8,128)(2,1)S(1)} all-to-all(bf16[16,96,384]{2,1,0:T(8,128)(2,1)S(1)} %shard_map.41), channel_id=1, replica_groups=mesh['x'=4,'y'=4,'z'=8,'core'=2] {'x','y'}, dimensions={0} | all-to-all | bytes 2359296 | tf_op jit(solution)/shard_map/all_to_all | solution.py:20
  27.8 0.9 shard_map.42
  28.7 2.0 %collective-permute-start = (f32[72,384]{1,0:T(8,128)S(1)}, f32[72,384]{1,0:T(8,128)S(1)}, u32[]{:S(2)}, u32[]{:S(2)}) collective-permute-start(f32[72,384]{1,0:T(8,128)S(1)} %get-tuple-element.7), channel_id=1, source_target_pairs={{0,1},{1,0},{2,3},{3,2},{4,5},{5,4},{6,7},{7,6},{8,9},{9,8},{10,11... | collective-permute-start | bytes 331784 | tf_op jit(solution)/shard_map/ppermute | solution.py:24
  30.8 1.0 collective-permute-done.got
  31.8 23.0 %all_to_all.26.parts = bf16[8,72,384]{2,1,0:T(8,128)(2,1)S(1)} all-to-all(bf16[8,72,384]{2,1,0:T(8,128)(2,1)S(1)} %shard_map.43), channel_id=1, replica_groups=mesh['x'=4,'y'=4,'z'=8,'core'=2] {'z'}, dimensions={0} | all-to-all | bytes 884736 | tf_op jit(solution)/shard_map/all_to_all | solution.py:20
  54.7 0.1 shard_map.44.mine
  54.8 1.8 %collective-permute-start.1 = (f32[72,384]{1,0:T(8,128)S(1)}, f32[72,384]{1,0:T(8,128)S(1)}, u32[]{:S(2)}, u32[]{:S(2)}) collective-permute-start(f32[72,384]{1,0:T(8,128)S(1)} %shard_map.44.mine), channel_id=1, source_target_pairs={{0,1},{1,0},{2,3},{3,2},{4,5},{5,4},{6,7},{7,6},{8,9},{9,8},{10,11... | collective-permute-start | bytes 331784 | tf_op jit(solution)/shard_map/ppermute | solution.py:24
  56.6 1.0 collective-permute-done.1.other
  57.6 3.9 %shard_map.45 = f32[16,48,128]{2,1,0:T(8,128)S(1)} custom-call(s32[1]{0:T(128)} %bitcast._.own, bf16[16,96,384]{2,1,0:T(8,128)(2,1)S(1)} %all_to_all.25.mixed, f32[72,384]{1,0:T(8,128)S(1)} %shard_map.44.mine, f32[72,384]{1,0:T(8,128)S(1)} %collective-permute-done.1.other), custom_call_target="tpu_custom_call" | custom-call | tf_op jit(solution)/shard_map/pallas_call | solution.py:317
  61.5 12.4 %all_to_all.27 = f32[16,48,128]{2,1,0:T(8,128)S(1)} all-to-all(f32[16,48,128]{2,1,0:T(8,128)S(1)} %shard_map.45), channel_id=1, replica_groups=mesh['x'=4,'y'=4,'z'=8,'core'=2] {'x','y'}, dimensions={0} | all-to-all | bytes 786432 | tf_op jit(solution)/shard_map/all_to_all | solution.py:20
  74.0 11.3 %all_to_all.28.powers = f32[16,48,128]{2,1,0:T(8,128)S(1)} all-to-all(f32[16,48,128]{2,1,0:T(8,128)S(1)} %broadcast_in_dim.3), channel_id=1, replica_groups=mesh['x'=4,'y'=4,'z'=8,'core'=2] {'x','y'}, dimensions={0} | all-to-all | bytes 786432 | tf_op jit(solution)/shard_map/all_to_all | solution.py:20
  85.2 1.0 shard_map.46
  86.2 3.0 %collective-permute-start.2 = (f32[240,128]{1,0:T(8,128)S(1)}, f32[240,128]{1,0:T(8,128)S(1)}, u32[]{:S(2)}, u32[]{:S(2)}) collective-permute-start(f32[240,128]{1,0:T(8,128)S(1)} %get-tuple-element.9), channel_id=1, source_target_pairs={{0,1},{1,0},{2,3},{3,2},{4,5},{5,4},{6,7},{7,6},{8,9},{9,8},{10,11... | collective-permute-start | bytes 368648 | tf_op jit(solution)/shard_map/ppermute | solution.py:24
  89.2 1.0 collective-permute-done.2.got
  90.2 15.0 %all_to_all.29.parts = f32[8,72,128]{2,1,0:T(8,128)S(1)} all-to-all(f32[8,72,128]{2,1,0:T(8,128)S(1)} %shard_map.47), channel_id=1, replica_groups=mesh['x'=4,'y'=4,'z'=8,'core'=2] {'z'}, dimensions={0} | all-to-all | bytes 589824 | tf_op jit(solution)/shard_map/all_to_all | solution.py:20
  105.2 4.0 %shard_map.48 = (f32[64,96]{1,0:T(8,128)}, f32[24,96]{1,0:T(8,128)}) custom-call(f32[8,72,128]{2,1,0:T(8,128)S(1)} %all_to_all.29.parts, f32[48,128]{1,0:T(8,128)S(1)} %reduce_sum.9.power), custom_call_target="tpu_custom_call" | custom-call | tf_op jit(solution)/shard_map/pallas_call | solution.py:383
  (4 shorter events, 0.1 us)
Async XLA Ops:
  28.7 3.0 %collective-permute-start = (f32[72,384]{1,0:T(8,128)S(1)}, f32[72,384]{1,0:T(8,128)S(1)}, u32[]{:S(2)}, u32[]{:S(2)}) collective-permute-start(f32[72,384]{1,0:T(8,128)S(1)} %get-tuple-element.7), channel_id=1, source_target_pairs={{0,1},{1,0},{2,3},{3,2},{4,5},{5,4},{6,7},{7,6},{8,9},{9,8},{10,11... | collective-permute-start | bytes 331784 | tf_op jit(solution)/shard_map/ppermute | solution.py:24
  54.8 2.8 %collective-permute-start.1 = (f32[72,384]{1,0:T(8,128)S(1)}, f32[72,384]{1,0:T(8,128)S(1)}, u32[]{:S(2)}, u32[]{:S(2)}) collective-permute-start(f32[72,384]{1,0:T(8,128)S(1)} %shard_map.44.mine), channel_id=1, source_target_pairs={{0,1},{1,0},{2,3},{3,2},{4,5},{5,4},{6,7},{7,6},{8,9},{9,8},{10,11... | collective-permute-start | bytes 331784 | tf_op jit(solution)/shard_map/ppermute | solution.py:24
  86.2 4.0 %collective-permute-start.2 = (f32[240,128]{1,0:T(8,128)S(1)}, f32[240,128]{1,0:T(8,128)S(1)}, u32[]{:S(2)}, u32[]{:S(2)}) collective-permute-start(f32[240,128]{1,0:T(8,128)S(1)} %get-tuple-element.9), channel_id=1, source_target_pairs={{0,1},{1,0},{2,3},{3,2},{4,5},{5,4},{6,7},{7,6},{8,9},{9,8},{10,11... | collective-permute-start | bytes 368648 | tf_op jit(solution)/shard_map/ppermute | solution.py:24
